TPU v7x, 128 devices: a whole 4x4x4 slice. The times are simulated.
128 devices in a mesh: seq: 8 (over z, y_hi), var: 16 (over y_lo, x, core).
Axes of the slice: x: 4, y: 4 (y_hi: 2, y_lo: 2; y = y_hi * 2 + y_lo), z: 4, core: 2. Of those that a mesh axis runs over, the one named last changes fastest.
Arguments:
- fields: float32 [48, 16, 1, 2048], P('var', None, None, 'seq'), may hold values from -6 to 6
- channel_ids: int32 [48], P('var'), may hold values from 0 to 47, each once
- lead_index: int32 [1], replicated, may hold values from 0 to 14
- embed_weight: bfloat16 [48, 16, 1024], P('var'), may hold values from -2 to 2
- var_table: bfloat16 [48, 1024], replicated, may hold values from -6 to 6
- agg_query: bfloat16 [16, 64], replicated, may hold values from -6 to 6
- agg_kv: bfloat16 [1024, 2, 1024], replicated, may hold values from -1 to 1
- agg_out: bfloat16 [1024, 1024], replicated, may hold values from -1 to 1
- agg_temp: float32 [16], replicated, may hold values from 2 to 8
- pos_table: bfloat16 [2048, 1024], P('seq'), may hold values from -6 to 6
- lead_table: bfloat16 [16, 1024], replicated, may hold values from -6 to 6
- norm_gain: float32 [2, 2, 1024], replicated, may hold values from 0.25 to 1.75
- qkv_weight: bfloat16 [2, 1024, 16, 192], P(None, None, 'var'), may hold values from -0.1875 to 0.1875
- attn_temp: float32 [2, 16], P(None, 'var'), may hold values from 2 to 8
- out_weight: bfloat16 [2, 16, 64, 1024], P(None, 'var'), may hold values from -0.1875 to 0.1875
- up_weight: bfloat16 [2, 1024, 4096], P(None, None, 'var'), may hold values from -0.1875 to 0.1875
- down_weight: bfloat16 [2, 4096, 1024], P(None, 'var'), may hold values from -0.09375 to 0.09375
- final_gain: float32 [1024], replicated, may hold values from 0.25 to 1.75
- head_weight: bfloat16 [1024, 48, 16], replicated, may hold values from -1 to 1
Outputs:
- forecast: float32 [2, 48, 16, 1, 2048], P(None, 'var', None, None, 'seq')
Inputs may be any that keep to these rules, and one draw needn't show every extreme that they name: `channel_ids`: each channel names its own row of var_table, every row once. lead_index + 1 names a row of lead_table.
All inputs are finite; a program needn't handle non-finite values.
Results may differ from a plain program's by a relative error of at most 0.006.
Values may be sent and summed in bfloat16 or wider, within the bound.
A program may use at most 128 MiB of HBM per device.

v0:
```python
import jax
import jax.numpy as jnp
from jax import lax
from jax.sharding import PartitionSpec as P

STEPS = 2


EPS_NORM = 1e-05
EPS_UNIT = 1e-06


def from_everyone(shard, axis):
    count = lax.axis_size(axis)
    return lax.all_to_all(
        jnp.broadcast_to(shard[None], (count, *shard.shape)), axis, 0, 0, tiled=True
    )


def in_order(pieces, dim):
    pieces = jnp.moveaxis(pieces, 0, dim)
    lengths = pieces.shape
    return pieces.reshape(*lengths[:dim], lengths[dim] * lengths[dim + 1], *lengths[dim + 2 :])


def collect(shard, axis, dim):
    pieces = from_everyone(shard, axis)
    return in_order(pieces, dim)


def split_up(shard, dim, count):
    before, after = (shard.shape[:dim], shard.shape[dim + 1 :])
    return jnp.moveaxis(shard.reshape(*before, count, -1, *after), dim, 0)


def sent_and_summed(shard, axis, dim):
    pieces = split_up(shard, dim, lax.axis_size(axis))
    arrived = lax.all_to_all(pieces, axis, split_axis=0, concat_axis=0, tiled=True)
    return arrived.sum(axis=0)


def side_by_side(arrays, axis, dim, along):
    columns = [a.reshape(*a.shape[:along], -1) for a in arrays]
    both = jnp.concatenate(columns, axis=along)
    out, at, outs = (lax.psum_scatter(both, axis, scatter_dimension=dim, tiled=True), 0, [])
    for a, column in zip(arrays, columns):
        section = out[..., at : at + column.shape[along]]
        outs.append(section.reshape(*section.shape[:along], *a.shape[along:]))
        at += column.shape[along]
    return tuple(outs)


def unit_rows(values):
    return values * lax.rsqrt(jnp.mean(values * values, axis=-1, keepdims=True) + EPS_UNIT)


def layer_norm(values, gain):
    centre = values - jnp.mean(values, axis=-1, keepdims=True)
    spread = jnp.mean(centre * centre, axis=-1, keepdims=True)
    return centre * lax.rsqrt(spread + EPS_NORM) * gain


def spread_rows(normed, matrix):
    return jnp.dot(collect(normed, "var", 0), matrix, preferred_element_type=jnp.float32)


def sum_rows(left, matrix):
    return sent_and_summed(jnp.dot(left, matrix, preferred_element_type=jnp.float32), "var", 0)


def per_device(
    fields,
    channel_ids,
    lead_index,
    embed_weight,
    var_table,
    agg_query,
    agg_kv,
    agg_out,
    agg_temp,
    pos_table,
    lead_table,
    norm_gain,
    qkv_weight,
    attn_temp,
    out_weight,
    up_weight,
    down_weight,
    final_gain,
    head_weight,
):
    var_count = lax.axis_size("var")
    var_place = lax.axis_index("var")
    local_vars, pixels, batch, local_patches = fields.shape
    total_vars, width = var_table.shape
    all_heads = agg_query.shape[0]
    head_width = agg_query.shape[1]
    heads_here = qkv_weight.shape[2]
    layer_count = qkv_weight.shape[0]
    lead_count = lead_table.shape[0]
    local_rows = batch * local_patches
    owned_rows = local_rows // var_count
    row_start = var_place * owned_rows
    ident_vars = (channel_ids[:, None] == jnp.arange(total_vars, dtype=jnp.int32)[None, :]).astype(
        jnp.bfloat16
    )
    var_rows = jnp.dot(ident_vars, var_table, preferred_element_type=jnp.float32)
    query_unit = unit_rows(agg_query.astype(jnp.float32))
    kv_mat = agg_kv.reshape(width, 2 * width)
    pos_rows = lax.dynamic_slice_in_dim(
        jnp.tile(pos_table, (batch, 1)), row_start, owned_rows, 0
    ).astype(jnp.float32)
    row_batch = (row_start + jnp.arange(owned_rows, dtype=jnp.int32)) // local_patches
    batch_hot = (row_batch[:, None] == jnp.arange(batch, dtype=jnp.int32)[None, :]).astype(
        jnp.int32
    )
    row_lead = jnp.sum(batch_hot * lead_index[None, :], axis=1)
    lead_iota = jnp.arange(lead_count, dtype=jnp.int32)
    state = fields
    outputs = []
    for step in range(STEPS):
        flat = state.astype(jnp.bfloat16).reshape(local_vars, pixels, local_rows)
        tokens = jnp.einsum("vkr,vkd->vrd", flat, embed_weight, preferred_element_type=jnp.float32)
        tokens = (tokens + var_rows[:, None, :]).astype(jnp.bfloat16)
        keyval = jnp.dot(
            tokens.reshape(local_vars * local_rows, width),
            kv_mat,
            preferred_element_type=jnp.float32,
        )
        keyval = keyval.reshape(local_vars, local_rows, 2, all_heads, head_width)
        key_unit = unit_rows(keyval[:, :, 0])
        affinity_raw = jnp.sum(key_unit * query_unit, axis=-1) * agg_temp / head_width
        score_exponent = jnp.exp(affinity_raw)
        numer = jnp.sum(score_exponent[..., None] * keyval[:, :, 1], axis=0)
        denom = jnp.sum(score_exponent, axis=0)
        numer, denom = side_by_side((numer, denom), "var", 0, 2)
        pooled = (numer / denom[:, :, None]).reshape(owned_rows, width).astype(jnp.bfloat16)
        lead_hot = ((row_lead + step)[:, None] == lead_iota[None, :]).astype(jnp.bfloat16)
        resid = jnp.dot(pooled, agg_out, preferred_element_type=jnp.float32) + pos_rows
        resid = resid + jnp.dot(lead_hot, lead_table, preferred_element_type=jnp.float32)
        for layer in range(layer_count):
            normed = layer_norm(resid, norm_gain[layer, 0]).astype(jnp.bfloat16)
            mixed = spread_rows(
                normed, qkv_weight[layer].reshape(width, heads_here * 3 * head_width)
            )
            mixed = mixed.reshape(batch, local_patches, heads_here, 3 * head_width)
            queries = unit_rows(mixed[..., :head_width]).astype(jnp.bfloat16)
            keys = unit_rows(mixed[..., head_width : 2 * head_width]).astype(jnp.bfloat16)
            values = mixed[..., 2 * head_width :].astype(jnp.bfloat16)
            packed = jnp.concatenate(
                [
                    keys.reshape(batch, local_patches, heads_here * head_width),
                    values.reshape(batch, local_patches, heads_here * head_width),
                ],
                axis=-1,
            )
            scale = attn_temp[layer] / head_width
            piece = collect(packed, "seq", 1)
            count = piece.shape[1]
            key_piece = piece[..., : heads_here * head_width].reshape(
                batch, count, heads_here, head_width
            )
            value_piece = piece[..., heads_here * head_width :].reshape(
                batch, count, heads_here, head_width
            )
            score_a = jnp.einsum(
                "bqhd,bkhd->bhqk", queries, key_piece, preferred_element_type=jnp.float32
            )
            expo_a = jnp.exp(score_a * scale[None, :, None, None])
            denom_a = jnp.sum(expo_a, axis=-1)
            numer_a = jnp.einsum(
                "bhqk,bkhd->bqhd",
                expo_a.astype(jnp.bfloat16),
                value_piece,
                preferred_element_type=jnp.float32,
            )
            numer_a, denom_a = (numer_a, denom_a)
            attended = numer_a / jnp.transpose(denom_a, (0, 2, 1))[..., None]
            attended = attended.astype(jnp.bfloat16).reshape(local_rows, heads_here * head_width)
            resid = resid + sum_rows(
                attended, out_weight[layer].reshape(heads_here * head_width, width)
            )
            normed = layer_norm(resid, norm_gain[layer, 1]).astype(jnp.bfloat16)
            hidden = jax.nn.gelu(spread_rows(normed, up_weight[layer]), approximate=False).astype(
                jnp.bfloat16
            )
            resid = resid + sum_rows(hidden, down_weight[layer])
        final = layer_norm(resid, final_gain).astype(jnp.bfloat16)
        own_head = lax.dynamic_slice_in_dim(
            head_weight, var_place * local_vars, local_vars, 1
        ).reshape(width, local_vars * pixels)
        delta = jnp.dot(collect(final, "var", 0), own_head, preferred_element_type=jnp.float32)
        delta = jnp.transpose(delta.reshape(batch, local_patches, local_vars, pixels), (2, 3, 0, 1))
        state = state + delta
        outputs.append(state)
    return jnp.stack(outputs)


def solution(mesh):
    return jax.shard_map(
        per_device,
        mesh=mesh,
        in_specs=(
            P("var", None, None, "seq"),
            P("var"),
            P(),
            P("var", None, None),
            P(),
            P(),
            P(),
            P(),
            P(),
            P("seq", None),
            P(),
            P(),
            P(None, None, "var", None),
            P(None, "var"),
            P(None, "var", None, None),
            P(None, None, "var"),
            P(None, "var", None),
            P(),
            P(),
        ),
        out_specs=P(None, "var", None, None, "seq"),
        check_vma=False,
    )
```

profile of v0, /device:TPU:1, one launch (start us, length us, event | category | flops | bytes accessed | tf_op | source)
XLA Modules:
  0.0 608.0 jit_solution(13116425019877743669)
XLA Ops:
  6.5 5.7 copy.124
  12.3 6.5 %copy.100 = bf16[2048,1024]{1,0:T(8,128)(2,1)} copy(bf16[2048,1024]{0,1:T(8,128)(2,1)} %bitcast.326) | data formatting | bytes 8388608 | tf_op jit(solution)/shard_map/dot_general | solution.py:125
  19.2 8.7 %fusion.10 = f32[3,256,2,16,64]{1,4,3,2,0:T(8,128)} fusion(bf16[2,16,64,1024,1]{3,2,1,0,4:T(8,128)(2,1)} %bitcast.328, bf16[3,16,1024]{2,1,0:T(8,128)(2,1)S(1)} %copy-done.25, f32[3,1024]{1,0:T(4,128)S(1)} %fusion.162, bf16[3,16,1,256]{3,2,1,0:T(2,128)(2,1)S(1)} %convert_element_type.144), kind=kOutput, calls=%fused_computation.24 | convolution fusion | flops 3247964160 | bytes 10620928 | tf_op jit(solution)/shard_map/dot_general | solution.py:125
  28.0 2.5 multiply_reduce_fusion.3
  30.5 3.0 multiply_reduce_fusion.2
  34.1 2.0 copy.102
  38.0 61.9 %reduce-scatter.3.cloned.1.call-done = f32[16,16,65]{2,1,0:T(8,128)} async-done(((f32[256,16,65]{2,1,0:T(8,128)}), f32[16,16,65]{2,1,0:T(8,128)}) %reduce-scatter.3.cloned.1.call-update) | async-done | bytes 66576 | tf_op jit(solution)/shard_map/reduce_scatter | solution.py:45
  99.9 1.0 slice.189
  101.1 1.0 fusion.114
  102.2 1.2 convolution_add_fusion.3
  104.1 16.2 %all_to_all.110 = bf16[16,16,1024]{2,1,0:T(8,128)(2,1)S(1)} all-to-all(bf16[16,16,1024]{2,1,0:T(8,128)(2,1)S(1)} %broadcast_in_dim.36), channel_id=1, replica_groups=mesh['seq'=8,'var'=16] {'var'}, dimensions={0} | all-to-all | bytes 1048576 | tf_op jit(solution)/shard_map/all_to_all | solution.py:15
  121.7 6.5 %all-to-all-start.1 = ((bf16[8,1,256,128]{3,2,1,0:T(8,128)(2,1)}), bf16[8,1,256,128]{3,2,1,0:T(8,128)(2,1)S(1)}, u32[]{:S(2)}, u32[]{:S(2)}) async-start(bf16[8,1,256,128]{3,2,1,0:T(8,128)(2,1)} %broadcast_in_dim.38), calls=%async_computation.2 | async-start | bytes 1048576 | tf_op jit(solution)/shard_map/all_to_all | solution.py:15
  128.2 1.3 fusion.177
  130.2 7.7 %all-to-all-done.1 = bf16[8,1,256,128]{3,2,1,0:T(8,128)(2,1)S(1)} async-done(((bf16[8,1,256,128]{3,2,1,0:T(8,128)(2,1)}), bf16[8,1,256,128]{3,2,1,0:T(8,128)(2,1)S(1)}, u32[]{:S(2)}, u32[]{:S(2)}) %all-to-all-start.1) | async-done | bytes 524320 | tf_op jit(solution)/shard_map/all_to_all | solution.py:15
  139.6 20.8 %all_to_all.111 = f32[16,16,1024]{2,1,0:T(8,128)S(1)} all-to-all(f32[16,16,1024]{2,1,0:T(8,128)S(1)} %fusion.121), channel_id=1, replica_groups=mesh['seq'=8,'var'=16] {'var'}, dimensions={0} | all-to-all | bytes 2097152 | tf_op jit(solution)/shard_map/all_to_all | solution.py:38
  161.1 1.0 fusion.174
  163.1 13.5 %all_to_all.112 = bf16[16,16,1024]{2,1,0:T(8,128)(2,1)S(1)} all-to-all(bf16[16,16,1024]{2,1,0:T(8,128)(2,1)S(1)} %broadcast_in_dim.39), channel_id=1, replica_groups=mesh['seq'=8,'var'=16] {'var'}, dimensions={0} | all-to-all | bytes 1048576 | tf_op jit(solution)/shard_map/all_to_all | solution.py:15
  176.6 1.9 fusion.67
  178.9 19.7 %all_to_all.113 = f32[16,16,1024]{2,1,0:T(8,128)} all-to-all(f32[16,16,1024]{2,1,0:T(8,128)S(1)} %fusion.43), channel_id=1, replica_groups=mesh['seq'=8,'var'=16] {'var'}, dimensions={0} | all-to-all | bytes 2097152 | tf_op jit(solution)/shard_map/all_to_all | solution.py:38
  198.6 1.9 reduce_sum.458
  200.5 1.0 fusion.173
  201.8 13.5 %all_to_all.114 = bf16[16,16,1024]{2,1,0:T(8,128)(2,1)S(1)} all-to-all(bf16[16,16,1024]{2,1,0:T(8,128)(2,1)S(1)} %broadcast_in_dim.40), channel_id=1, replica_groups=mesh['seq'=8,'var'=16] {'var'}, dimensions={0} | all-to-all | bytes 1048576 | tf_op jit(solution)/shard_map/all_to_all | solution.py:15
  215.3 1.3 convolution_bitcast_fusion.2
  219.8 4.1 all-to-all-start.6
  225.2 9.1 %all-to-all-done.6 = bf16[8,1,256,128]{3,2,1,0:T(8,128)(2,1)} async-done(((bf16[8,1,256,128]{3,2,1,0:T(8,128)(2,1)}), bf16[8,1,256,128]{3,2,1,0:T(8,128)(2,1)}, u32[]{:S(2)}, u32[]{:S(2)}) %all-to-all-start.6) | async-done | bytes 524320 | tf_op jit(solution)/shard_map/all_to_all | solution.py:15
  234.2 1.7 fusion.180
  235.9 2.3 fusion.26
  239.4 20.8 %all_to_all.115 = f32[16,16,1024]{2,1,0:T(8,128)} all-to-all(f32[16,16,1024]{2,1,0:T(8,128)S(1)} %fusion.117), channel_id=1, replica_groups=mesh['seq'=8,'var'=16] {'var'}, dimensions={0} | all-to-all | bytes 2097152 | tf_op jit(solution)/shard_map/all_to_all | solution.py:38
  260.2 1.9 reduce_sum.464
  263.4 13.5 %all_to_all.116 = bf16[16,16,1024]{2,1,0:T(8,128)(2,1)S(1)} all-to-all(bf16[16,16,1024]{2,1,0:T(8,128)(2,1)S(1)} %broadcast_in_dim.43), channel_id=1, replica_groups=mesh['seq'=8,'var'=16] {'var'}, dimensions={0} | all-to-all | bytes 1048576 | tf_op jit(solution)/shard_map/all_to_all | solution.py:15
  276.9 1.8 fusion.70
  279.0 19.1 %all_to_all.117 = f32[16,16,1024]{2,1,0:T(8,128)S(1)} all-to-all(f32[16,16,1024]{2,1,0:T(8,128)S(1)} %fusion.35), channel_id=1, replica_groups=mesh['seq'=8,'var'=16] {'var'}, dimensions={0} | all-to-all | bytes 2097152 | tf_op jit(solution)/shard_map/all_to_all | solution.py:38
  300.1 4.8 all-to-all-start.10
  305.0 9.6 %all-to-all-done.10 = bf16[16,16,1024]{2,1,0:T(8,128)(2,1)S(1)} async-done(((bf16[16,16,1024]{2,1,0:T(8,128)(2,1)}), bf16[16,16,1024]{2,1,0:T(8,128)(2,1)S(1)}, u32[]{:S(2)}, u32[]{:S(2)}) %all-to-all-start.10) | async-done | bytes 524320 | tf_op jit(solution)/shard_map/all_to_all | solution.py:15
  314.5 1.2 fusion.24
  315.7 8.8 %fusion.8 = f32[3,256,2,16,64]{1,4,3,2,0:T(8,128)} fusion(bf16[2,16,64,1024,1]{3,2,1,0,4:T(8,128)(2,1)} %bitcast.329, bf16[3,16,1024]{2,1,0:T(8,128)(2,1)} %param.22, f32[3,1024]{1,0:T(4,128)} %copy-done.27, f32[3,16,1,256]{3,1,0,2:T(8,128)S(1)} %fusion.24), kind=kOutput, calls=%fused_computation.22 | convolution fusion | flops 3247976448 | bytes 10645504 | tf_op jit(solution)/shard_map/dot_general | solution.py:125
  324.5 2.5 multiply_reduce_fusion.1
  327.0 3.0 multiply_reduce_fusion
  330.6 2.0 copy.111
  332.7 56.6 %reduce-scatter.5.cloned.1.call-done = f32[16,16,65]{2,1,0:T(8,128)} async-done(((f32[256,16,65]{2,1,0:T(8,128)}), f32[16,16,65]{2,1,0:T(8,128)}) %reduce-scatter.5.cloned.1.call-update) | async-done | bytes 66576 | tf_op jit(solution)/shard_map/reduce_scatter | solution.py:45
  389.3 1.0 slice.203
  390.5 1.0 fusion.113
  391.6 1.1 convolution_add_fusion.1
  393.4 16.3 %all_to_all.118 = bf16[16,16,1024]{2,1,0:T(8,128)(2,1)S(1)} all-to-all(bf16[16,16,1024]{2,1,0:T(8,128)(2,1)S(1)} %broadcast_in_dim.45), channel_id=1, replica_groups=mesh['seq'=8,'var'=16] {'var'}, dimensions={0} | all-to-all | bytes 1048576 | tf_op jit(solution)/shard_map/all_to_all | solution.py:15
  411.1 6.3 %all-to-all-start.12 = ((bf16[8,1,256,128]{3,2,1,0:T(8,128)(2,1)}), bf16[8,1,256,128]{3,2,1,0:T(8,128)(2,1)S(1)}, u32[]{:S(2)}, u32[]{:S(2)}) async-start(bf16[8,1,256,128]{3,2,1,0:T(8,128)(2,1)} %broadcast_in_dim.47), calls=%async_computation.14 | async-start | bytes 1048576 | tf_op jit(solution)/shard_map/all_to_all | solution.py:15
  417.4 9.7 %all-to-all-done.12 = bf16[8,1,256,128]{3,2,1,0:T(8,128)(2,1)S(1)} async-done(((bf16[8,1,256,128]{3,2,1,0:T(8,128)(2,1)}), bf16[8,1,256,128]{3,2,1,0:T(8,128)(2,1)S(1)}, u32[]{:S(2)}, u32[]{:S(2)}) %all-to-all-start.12) | async-done | bytes 524320 | tf_op jit(solution)/shard_map/all_to_all | solution.py:15
  428.8 20.9 %all_to_all.119 = f32[16,16,1024]{2,1,0:T(8,128)S(1)} all-to-all(f32[16,16,1024]{2,1,0:T(8,128)S(1)} %fusion.119), channel_id=1, replica_groups=mesh['seq'=8,'var'=16] {'var'}, dimensions={0} | all-to-all | bytes 2097152 | tf_op jit(solution)/shard_map/all_to_all | solution.py:38
  451.7 13.5 %all_to_all.120 = bf16[16,16,1024]{2,1,0:T(8,128)(2,1)S(1)} all-to-all(bf16[16,16,1024]{2,1,0:T(8,128)(2,1)S(1)} %broadcast_in_dim.48), channel_id=1, replica_groups=mesh['seq'=8,'var'=16] {'var'}, dimensions={0} | all-to-all | bytes 1048576 | tf_op jit(solution)/shard_map/all_to_all | solution.py:15
  465.1 1.9 fusion.73
  467.4 19.7 %all_to_all.121 = f32[16,16,1024]{2,1,0:T(8,128)} all-to-all(f32[16,16,1024]{2,1,0:T(8,128)S(1)} %fusion.41), channel_id=1, replica_groups=mesh['seq'=8,'var'=16] {'var'}, dimensions={0} | all-to-all | bytes 2097152 | tf_op jit(solution)/shard_map/all_to_all | solution.py:38
  487.1 1.9 reduce_sum.482
  490.4 13.5 %all_to_all.122 = bf16[16,16,1024]{2,1,0:T(8,128)(2,1)S(1)} all-to-all(bf16[16,16,1024]{2,1,0:T(8,128)(2,1)S(1)} %broadcast_in_dim.49), channel_id=1, replica_groups=mesh['seq'=8,'var'=16] {'var'}, dimensions={0} | all-to-all | bytes 1048576 | tf_op jit(solution)/shard_map/all_to_all | solution.py:15
  503.8 1.3 convolution_bitcast_fusion
  508.3 4.4 all-to-all-start.17
  512.7 10.0 %all-to-all-done.17 = bf16[8,1,256,128]{3,2,1,0:T(8,128)(2,1)} async-done(((bf16[8,1,256,128]{3,2,1,0:T(8,128)(2,1)}), bf16[8,1,256,128]{3,2,1,0:T(8,128)(2,1)}, u32[]{:S(2)}, u32[]{:S(2)}) %all-to-all-start.17) | async-done | bytes 524320 | tf_op jit(solution)/shard_map/all_to_all | solution.py:15
  522.7 1.7 fusion.183
  524.4 2.3 fusion.28
  527.9 20.8 %all_to_all.123 = f32[16,16,1024]{2,1,0:T(8,128)} all-to-all(f32[16,16,1024]{2,1,0:T(8,128)S(1)} %fusion.115), channel_id=1, replica_groups=mesh['seq'=8,'var'=16] {'var'}, dimensions={0} | all-to-all | bytes 2097152 | tf_op jit(solution)/shard_map/all_to_all | solution.py:38
  548.7 1.3 reduce_sum.488
  550.5 13.5 %all_to_all.124 = bf16[16,16,1024]{2,1,0:T(8,128)(2,1)S(1)} all-to-all(bf16[16,16,1024]{2,1,0:T(8,128)(2,1)S(1)} %broadcast_in_dim.52), channel_id=1, replica_groups=mesh['seq'=8,'var'=16] {'var'}, dimensions={0} | all-to-all | bytes 1048576 | tf_op jit(solution)/shard_map/all_to_all | solution.py:15
  564.0 1.8 fusion.76
  566.1 19.1 %all_to_all.125 = f32[16,16,1024]{2,1,0:T(8,128)S(1)} all-to-all(f32[16,16,1024]{2,1,0:T(8,128)S(1)} %fusion.33), channel_id=1, replica_groups=mesh['seq'=8,'var'=16] {'var'}, dimensions={0} | all-to-all | bytes 2097152 | tf_op jit(solution)/shard_map/all_to_all | solution.py:38
  585.8 13.5 %all_to_all.126 = bf16[16,16,1024]{2,1,0:T(8,128)(2,1)S(1)} all-to-all(bf16[16,16,1024]{2,1,0:T(8,128)(2,1)S(1)} %broadcast_in_dim.53), channel_id=1, replica_groups=mesh['seq'=8,'var'=16] {'var'}, dimensions={0} | all-to-all | bytes 1048576 | tf_op jit(solution)/shard_map/all_to_all | solution.py:15
  599.2 1.2 fusion.23
  (195 shorter events, 31.7 us)
Async XLA Ops:
  6.5 95.7 %copy-start = (bf16[1024,1024]{1,0:T(8,128)(2,1)S(1)}, bf16[1024,1024]{1,0:T(8,128)(2,1)}, u32[]{:S(2)}) copy-start(bf16[1024,1024]{1,0:T(8,128)(2,1)} %param.26) | copy-start | bytes 6291460
  6.5 93.4 %reduce-scatter.3.cloned.1.call-start = ((), (), s32[]{:S(2)}) async-start(), calls=%async_computation.24 | async-start | bytes 2228224 | tf_op jit(solution)/shard_map/reduce_scatter | solution.py:45
  12.2 6.5 %copy-start.12 = (f32[3,16,1,256]{3,2,1,0:T(1,128)S(1)}, f32[3,16,1,256]{3,2,1,0:T(1,128)}, u32[]{:S(2)}) copy-start(f32[3,16,1,256]{3,2,1,0:T(1,128)} %param.19) | copy-start | bytes 147460
  12.2 6.6 %copy-start.19 = (bf16[16,64]{1,0:T(8,128)(2,1)S(1)}, bf16[16,64]{1,0:T(8,128)(2,1)}, u32[]{:S(2)}) copy-start(bf16[16,64]{1,0:T(8,128)(2,1)} %param.24) | copy-start | bytes 6148
  12.2 6.8 %copy-start.24 = (bf16[48,1024]{1,0:T(8,128)(2,1)S(1)}, bf16[48,1024]{1,0:T(8,128)(2,1)}, u32[]{:S(2)}) copy-start(bf16[48,1024]{1,0:T(8,128)(2,1)} %param.23) | copy-start | bytes 294916
  12.2 6.8 %copy-start.26 = (s32[3]{0:T(128)S(1)}, s32[3]{0:T(128)}, u32[]{:S(2)}) copy-start(s32[3]{0:T(128)} %param.20) | copy-start | bytes 40
  12.2 7.0 %copy-start.25 = (bf16[3,16,1024]{2,1,0:T(8,128)(2,1)S(1)}, bf16[3,16,1024]{2,1,0:T(8,128)(2,1)}, u32[]{:S(2)}) copy-start(bf16[3,16,1024]{2,1,0:T(8,128)(2,1)} %param.22) | copy-start | bytes 294916
  19.2 8.8 %copy-start.27 = (f32[3,1024]{1,0:T(4,128)}, f32[3,1024]{1,0:T(4,128)S(1)}, u32[]{:S(2)}) copy-start(f32[3,1024]{1,0:T(4,128)S(1)} %fusion.162) | copy-start | bytes 36868
  28.0 5.5 copy-start.21
  28.0 5.6 copy-start.2
  34.1 3.3 copy-start.20
  36.1 67.3 %copy-start.13 = (bf16[16,1024]{1,0:T(8,128)(2,1)S(1)}, bf16[16,1024]{1,0:T(8,128)(2,1)}, u32[]{:S(2)}) copy-start(bf16[16,1024]{1,0:T(8,128)(2,1)} %param.29) | copy-start | bytes 98308
  36.1 84.2 %copy-start.5 = (bf16[2,1024,1,192]{1,3,2,0:T(8,128)(2,1)S(1)}, bf16[2,1024,1,192]{1,3,2,0:T(8,128)(2,1)}, u32[]{:S(2)}) copy-start(bf16[2,1024,1,192]{1,3,2,0:T(8,128)(2,1)} %param.31) | copy-start | bytes 2359300
  38.0 82.3 %copy-start.16 = (f32[1,1,1024]{2,1,0:T(1,128)}, f32[1,1,1024]{2,1,0:T(1,128)S(1)}, u32[]{:S(2)}) copy-start(f32[1,1,1024]{2,1,0:T(1,128)S(1)} %get-tuple-element.37) | copy-start | bytes 12292
  120.6 18.7 %copy-start.7 = (bf16[2,1,64,1024]{3,2,1,0:T(8,128)(2,1)S(1)}, bf16[2,1,64,1024]{3,2,1,0:T(8,128)(2,1)}, u32[]{:S(2)}) copy-start(bf16[2,1,64,1024]{3,2,1,0:T(8,128)(2,1)} %param.33) | copy-start | bytes 786436
  121.7 16.2 %all-to-all-start.1 = ((bf16[8,1,256,128]{3,2,1,0:T(8,128)(2,1)}), bf16[8,1,256,128]{3,2,1,0:T(8,128)(2,1)S(1)}, u32[]{:S(2)}, u32[]{:S(2)}) async-start(bf16[8,1,256,128]{3,2,1,0:T(8,128)(2,1)} %broadcast_in_dim.38), calls=%async_computation.2 | async-start | bytes 1048576 | tf_op jit(solution)/shard_map/all_to_all | solution.py:15
  176.6 1.9 copy-start.3
  216.6 0.7 copy-start.8
  219.8 14.4 %all-to-all-start.6 = ((bf16[8,1,256,128]{3,2,1,0:T(8,128)(2,1)}), bf16[8,1,256,128]{3,2,1,0:T(8,128)(2,1)}, u32[]{:S(2)}, u32[]{:S(2)}) async-start(bf16[8,1,256,128]{3,2,1,0:T(8,128)(2,1)} %broadcast_in_dim.42), calls=%async_computation.7 | async-start | bytes 1048576 | tf_op jit(solution)/shard_map/all_to_all | solution.py:15
  300.1 14.4 %all-to-all-start.10 = ((bf16[16,16,1024]{2,1,0:T(8,128)(2,1)}), bf16[16,16,1024]{2,1,0:T(8,128)(2,1)S(1)}, u32[]{:S(2)}, u32[]{:S(2)}) async-start(bf16[16,16,1024]{2,1,0:T(8,128)(2,1)} %broadcast_in_dim.44), calls=%async_computation.11 | async-start | bytes 1048576 | tf_op jit(solution)/shard_map/all_to_all | solution.py:15
  304.9 84.4 %reduce-scatter.5.cloned.1.call-start = ((), (), s32[]{:S(2)}) async-start(), calls=%async_computation.25 | async-start | bytes 2228224 | tf_op jit(solution)/shard_map/reduce_scatter | solution.py:45
  315.7 8.8 %copy-start.10 = (f32[3,16,1,256]{3,1,0,2:T(8,128)}, f32[3,16,1,256]{3,1,0,2:T(8,128)S(1)}, u32[]{:S(2)}) copy-start(f32[3,16,1,256]{3,1,0,2:T(8,128)S(1)} %fusion.24) | copy-start | bytes 147460
  324.5 5.5 copy-start.22
  324.5 5.6 copy-start.1
  332.6 60.1 %copy-start.14 = (bf16[16,1024]{1,0:T(8,128)(2,1)S(1)}, bf16[16,1024]{1,0:T(8,128)(2,1)}, u32[]{:S(2)}) copy-start(bf16[16,1024]{1,0:T(8,128)(2,1)} %param.29) | copy-start | bytes 98308
  332.6 60.1 %copy-start.23 = (s32[16]{0:T(128)S(1)}, s32[16]{0:T(128)}, u32[]{:S(2)}) copy-start(s32[16]{0:T(128)} %get-tuple-element.21) | copy-start | bytes 196
  332.7 60.6 %copy-start.17 = (f32[1,1,1024]{2,1,0:T(1,128)S(1)}, f32[1,1,1024]{2,1,0:T(1,128)}, u32[]{:S(2)}) copy-start(f32[1,1,1024]{2,1,0:T(1,128)} %copy-done.16) | copy-start | bytes 12292
  332.7 77.0 %copy-start.6 = (bf16[2,1024,1,192]{1,3,2,0:T(8,128)(2,1)S(1)}, bf16[2,1024,1,192]{1,3,2,0:T(8,128)(2,1)}, u32[]{:S(2)}) copy-start(bf16[2,1024,1,192]{1,3,2,0:T(8,128)(2,1)} %param.31) | copy-start | bytes 2359300
  411.1 16.0 %all-to-all-start.12 = ((bf16[8,1,256,128]{3,2,1,0:T(8,128)(2,1)}), bf16[8,1,256,128]{3,2,1,0:T(8,128)(2,1)S(1)}, u32[]{:S(2)}, u32[]{:S(2)}) async-start(bf16[8,1,256,128]{3,2,1,0:T(8,128)(2,1)} %broadcast_in_dim.47), calls=%async_computation.14 | async-start | bytes 1048576 | tf_op jit(solution)/shard_map/all_to_all | solution.py:15
  427.7 23.8 %copy-start.15 = (f32[1,1,1024]{2,1,0:T(1,128)S(1)}, f32[1,1,1024]{2,1,0:T(1,128)}, u32[]{:S(2)}) copy-start(f32[1,1,1024]{2,1,0:T(1,128)} %get-tuple-element.36) | copy-start | bytes 12292
  465.1 1.9 copy-start.4
  505.2 0.7 copy-start.9
  508.3 14.4 %all-to-all-start.17 = ((bf16[8,1,256,128]{3,2,1,0:T(8,128)(2,1)}), bf16[8,1,256,128]{3,2,1,0:T(8,128)(2,1)}, u32[]{:S(2)}, u32[]{:S(2)}) async-start(bf16[8,1,256,128]{3,2,1,0:T(8,128)(2,1)} %broadcast_in_dim.51), calls=%async_computation.19 | async-start | bytes 1048576 | tf_op jit(solution)/shard_map/all_to_all | solution.py:15
  565.8 19.8 %copy-start.18 = (f32[1024]{0:T(1024)S(1)}, f32[1024]{0:T(1024)}, u32[]{:S(2)}) copy-start(f32[1024]{0:T(1024)} %param.36) | copy-start | bytes 12292
  565.8 33.4 %copy-start.11 = (f32[3,16,1,256]{3,1,0,2:T(8,128)S(1)}, f32[3,16,1,256]{3,1,0,2:T(8,128)}, u32[]{:S(2)}) copy-start(f32[3,16,1,256]{3,1,0,2:T(8,128)} %copy-done.10) | copy-start | bytes 147460
Sparse Core Ops, SparseCore 0:
  36.2 63.6 reduce-scatter.2
  332.8 56.4 reduce-scatter.4
where the time goes:
time: 611 us; the launch traced here: 608 us
  blocking collectives  288 us (47%)
  waiting for transfers between devices  165 us (27%)
  matrix products  46.8 us (8%)
  other arithmetic  35.6 us (6%)
  local copies, waits for them, and re-layouts  31.1 us (5%)
  starting transfers between devices  26.1 us (4%)
  between operations  16.1 us (3%)
    all_to_all x8, blocking collectives, sent_and_summed(): lax.all_to_all(pieces, axis, split_axis=0, concat_axis=0, tiled=True)  161 us
    all_to_all x9, blocking collectives, from_everyone(): lax.all_to_all(jnp.broadcast_to(shard[None], (count, *shard.shape)), axis...  127 us
    reduce_scatter x2, waiting for transfers between devices, side_by_side(): lax.psum_scatter(both, axis, scatter_dimension=dim, tiled=True)  119 us
    all_to_all x5, waiting for transfers between devices, from_everyone(): lax.all_to_all(jnp.broadcast_to(shard[None], (count, *shard.shape)), axis...  46.1 us
    all_to_all x5, starting transfers between devices, from_everyone(): lax.all_to_all(jnp.broadcast_to(shard[None], (count, *shard.shape)), axis...  26.1 us
    dot_general x2, matrix products, per_device(): jnp.dot(tokens.reshape(local_vars * local_rows, width), kv_mat, preferred...  17.6 us
  transfers between devices with their start and end apart: 7, of which 7 were waited for; matrix products, arithmetic and copies ran while one was open for 1% of the time, Pallas kernels for 0%

commit v1 on v0

v1 whole, which is shorter than its diff:
```python
import jax
import jax.numpy as jnp
from jax import lax
from jax.experimental import pallas as pl
from jax.experimental.pallas import tpu as pltpu
from jax.sharding import PartitionSpec as P

STEPS = 2
LAYERS = 2
EPS_NORM = 1e-05
EPS_UNIT = 1e-06
F32 = jnp.float32
BF16 = jnp.bfloat16
MESH = pl.DeviceIdType.MESH

VAR_OFFS = ((2, 1), (1, 1), (3, 1), (2, 0), (0, 1), (1, 0), (3, 0))
SEQ_OFFS = ((2, 1), (1, 1), (3, 1), (0, 1), (2, 0), (1, 0), (3, 0))


def dot(a, b):
    return lax.dot_general(a, b, (((1,), (0,)), ((), ())), preferred_element_type=F32)


def dot_t(a, b):
    return lax.dot_general(a, b, (((1,), (1,)), ((), ())), preferred_element_type=F32)


def layer_norm(values, gain):
    centre = values - jnp.mean(values, axis=-1, keepdims=True)
    spread = jnp.mean(centre * centre, axis=-1, keepdims=True)
    return centre * lax.rsqrt(spread + EPS_NORM) * gain


def kernel(
    fields, ids, lead, emb, vart, aquery, kv_h, aout_h, atemp, pos_h, leadt, gains,
    qkv_h, temp, wo_h, up_h, dn_h, fgain, head_h,
    out,
    wq, wkv, wo, wu, wd, kvv, aout, headp, posv,
    fsnd, st, we, vr, vrt, mb, bb, kb, k2, vv, wb, nd, ndx, ndr, hexp, qexp,
    resid, xg, pb, rsb, qb, qx, kvb, kvo, ax, ab, fb, db, dlr,
    s_loc, s_ws, s_wr, s_is, s_ir, s_es, s_er, s_vs, s_vr, s_ag_s, s_ag_r, s_rs_s, s_rs_r,
    s_kv_s, s_kv_r, s_px_s, s_px_r, s_d_s, s_d_r,
):
    s = lax.axis_index("seq")
    v = lax.axis_index("var")
    i = v % 2
    p = v // 2
    px = p % 4
    py = p // 4
    sz = s // 2
    sy = s % 2
    other = (s, p * 2 + (1 - i))

    var_dst = []
    var_src = []
    for dx, dy in VAR_OFFS:
        var_dst.append(((py + dy) % 2) * 4 + (px + dx) % 4)
        var_src.append(((py + 2 - dy) % 2) * 4 + (px + 4 - dx) % 4)
    seq_dst = []
    seq_src = []
    for dz, dy in SEQ_OFFS:
        seq_dst.append(((sz + dz) % 4) * 2 + (sy + dy) % 2)
        seq_src.append(((sz + 4 - dz) % 4) * 2 + (sy + 2 - dy) % 2)

    def var_dev(q):
        return (s, q * 2 + i)

    def remote(src, dst, send, recv, dev):
        return pltpu.make_async_remote_copy(
            src_ref=src, dst_ref=dst, send_sem=send, recv_sem=recv, device_id=dev, device_id_type=MESH
        )

    own_heads = ((qkv_h.at[:, pl.ds(0, 64)], wq.at[i, :, pl.ds(0, 64)]),
                 (qkv_h.at[:, pl.ds(64, 128)], wkv.at[i]),
                 (wo_h, wo.at[i, :, pl.ds(64, 64)]),
                 (up_h, wu.at[i]),
                 (dn_h, wd.at[i]))
    loads = [pltpu.make_async_copy(kv_h, kvv, s_loc.at[0]),
             pltpu.make_async_copy(emb, we.at[p], s_loc.at[1]),
             pltpu.make_async_copy(aout_h, aout, s_loc.at[2]),
             pltpu.make_async_copy(pos_h.at[pl.ds(v * 16, 16)], posv, s_loc.at[3]),
             pltpu.make_async_copy(head_h.at[:, i], headp.at[:, pl.ds(0, 48)], s_loc.at[4])]
    for k, (a, b) in enumerate(own_heads):
        loads.append(pltpu.make_async_copy(a, b, s_loc.at[5 + k]))
    for c in loads:
        c.start()

    bar = pltpu.get_barrier_semaphore()
    for q in var_dst:
        pl.semaphore_signal(bar, inc=1, device_id=var_dev(q), device_id_type=MESH)
    for t in seq_dst:
        for j in range(2):
            pl.semaphore_signal(bar, inc=1, device_id=(t, p * 2 + j), device_id_type=MESH)
    pl.semaphore_signal(bar, inc=1, device_id=other, device_id_type=MESH)

    lane16 = lax.broadcasted_iota(jnp.int32, (32, 48), 1) // 16
    fpad = jnp.concatenate([fields[...], jnp.zeros((80, 256), F32)], axis=0)
    fsnd[...] = jnp.transpose(fpad).reshape(8, 32, 128)
    row8 = lax.broadcasted_iota(jnp.int32, (8, 48), 0)
    ch8 = lax.broadcasted_iota(jnp.int32, (8, 48), 1)
    named = jnp.where(row8 == 0, ids[0], jnp.where(row8 == 1, ids[1], ids[2]))
    hot = jnp.where((named == ch8) & (row8 < 3), 1.0, 0.0).astype(BF16)
    vrt[...] = dot(hot, vart[...]).astype(BF16)

    pl.semaphore_wait(bar, 22)

    init = []
    for k in range(7):
        init.append(remote(fsnd.at[var_dst[k]], st.at[p], s_is.at[k], s_ir.at[k], var_dev(var_dst[k])))
        init.append(remote(vrt, vr.at[p], s_vs.at[k], s_vr.at[k], var_dev(var_dst[k])))
        init.append(remote(emb, we.at[p], s_es.at[k], s_er.at[k], var_dev(var_dst[k])))
    for c in init:
        c.start()
    wcopies = []
    for k, (a, b) in enumerate(own_heads):
        wcopies.append(remote(a, b, s_ws.at[k], s_wr.at[k], other))
    for c in wcopies:
        c.start()

    st[p] = fsnd[p]
    vr[p] = vrt[...]
    wq[:, :, pl.ds(64, 64)] = jnp.zeros((2, LAYERS, 64, 1024), BF16)
    wo[:, :, pl.ds(0, 64)] = jnp.zeros((2, LAYERS, 64, 1024), BF16)
    headp[:, pl.ds(48, 80)] = jnp.zeros((8, 80, 1024), BF16)

    hrow = lax.broadcasted_iota(jnp.int32, (128, 1024), 0)
    hcol = lax.broadcasted_iota(jnp.int32, (128, 1024), 1) // 64
    hexp[...] = jnp.where(hrow == hcol, 1.0, 0.0).astype(BF16)
    aq = aquery[...].astype(F32)
    aq = aq * lax.rsqrt(jnp.mean(aq * aq, axis=-1, keepdims=True) + EPS_UNIT)
    aqt = jnp.concatenate([aq] * 16, axis=1)
    aqt = jnp.concatenate([aqt, jnp.zeros((112, 1024), F32)], axis=0)
    qexp[...] = jnp.where(hrow == hcol, aqt, 0.0).astype(BF16)
    tvec = jnp.concatenate([atemp[...] * (1.0 / 64.0), jnp.zeros((1, 112), F32)], axis=1)

    loads[0].wait()
    loads[1].wait()
    for k in range(7):
        remote(emb, we.at[var_src[k]], s_es.at[k], s_er.at[k], var_dev(var_dst[k])).wait_recv()
        remote(vrt, vr.at[var_src[k]], s_vs.at[k], s_vr.at[k], var_dev(var_dst[k])).wait_recv()

    wall = we[...].reshape(384, 1024)
    vall = vr[...].reshape(64, 1024)
    for n in range(4):
        cols = pl.ds(n * 512, 512)
        mb[:, :, cols] = dot(wall, kvv[:, cols]).astype(BF16).reshape(8, 48, 512)
        bb[:, :, cols] = dot(vall, kvv[:, cols]).reshape(8, 8, 512)
    for k in range(7):
        remote(fsnd.at[0], st.at[var_src[k]], s_is.at[k], s_ir.at[k], var_dev(var_dst[k])).wait_recv()
    for c in init:
        c.wait_send()
    for c in loads[2:5]:
        c.wait()

    lane128 = lax.broadcasted_iota(jnp.int32, (128, 128), 1)

    def partner(src, dst, k):
        return remote(src, dst, s_px_s.at[k], s_px_r.at[k], other)

    def gather_rows(normed, work):
        xg[p] = normed.astype(BF16)
        cs = [remote(xg.at[p], xg.at[p], s_ag_s.at[k], s_ag_r.at[k], var_dev(var_dst[k])) for k in range(7)]
        for c in cs:
            c.start()
        for k in range(7):
            remote(xg.at[p], xg.at[var_src[k]], s_ag_s.at[k], s_ag_r.at[k], var_dev(var_dst[k])).wait_recv()
        res = work(xg[...].reshape(128, 1024))
        for c in cs:
            c.wait_send()
        return res

    def sum_rows(part):
        pb[...] = part.astype(BF16).reshape(8, 16, 1024)
        cs = [remote(pb.at[var_dst[k]], rsb.at[k], s_rs_s.at[k], s_rs_r.at[k], var_dev(var_dst[k])) for k in range(7)]
        for c in cs:
            c.start()
        total = resid[...] + pb[p].astype(F32)
        for k in (6, 5, 4, 3, 2, 1, 0):
            cs[k].wait_recv()
            total = total + rsb[k].astype(F32)
        resid[...] = total
        for c in cs:
            c.wait_send()

    def step_body(step, carry):
        def pool_keys(q, c):
            sb = st[q][:, :48]
            blk = jnp.concatenate([jnp.where(lane16 == n, sb, 0.0) for n in range(3)], axis=0).astype(BF16)
            bias = bb[q]
            brow = jnp.concatenate([jnp.broadcast_to(bias[n:n + 1], (32, 2048)) for n in range(3)], axis=0)
            kk = dot(blk, mb[q, :, pl.ds(0, 1024)]) + brow[:, :1024]
            kb[q] = kk.astype(BF16)
            k2[q] = (kk * kk).astype(BF16)
            vv[q] = dot(blk, mb[q, :, pl.ds(1024, 1024)]) + brow[:, 1024:]
            return c

        lax.fori_loop(0, 8, pool_keys, 0)
        ss = dot_t(k2[...].reshape(768, 1024), hexp[...])
        qk = dot_t(kb[...].reshape(768, 1024), qexp[...])
        w = jnp.exp(qk * lax.rsqrt(ss * (1.0 / 64.0) + EPS_UNIT) * tvec)
        wb[...] = w.astype(BF16).reshape(8, 96, 128)
        nd[...] = jnp.zeros((32, 2048), F32)

        def pool_sum(q, c):
            wx = dot(wb[q], hexp[...])
            num = wx * vv[q]
            nd[:, pl.ds(0, 1024)] = nd[:, pl.ds(0, 1024)] + (num[0:32] + num[32:64] + num[64:96])
            nd[:, pl.ds(1024, 1024)] = nd[:, pl.ds(1024, 1024)] + (wx[0:32] + wx[32:64] + wx[64:96])
            return c

        lax.fori_loop(0, 8, pool_sum, 0)
        ndx[...] = nd[...].reshape(2, 16, 2048)
        c = partner(ndx.at[1 - i], ndr, 0)
        c.start()
        row16 = lax.broadcasted_iota(jnp.int32, (16, 16), 1)
        lhot = jnp.where(row16 == lead[0] + step, 1.0, 0.0).astype(BF16)
        add = posv[...].astype(F32) + dot(lhot, leadt[...])
        c.wait_recv()
        tot = ndx[i] + ndr[...]
        pooled = (tot[:, :1024] / tot[:, 1024:]).astype(BF16)
        c.wait_send()
        resid[...] = dot(pooled, aout[...]) + add

        @pl.when(step == 0)
        def _():
            for c in loads[5:]:
                c.wait()
            for c in wcopies:
                c.wait()

        def layer_body(l, carry):
            def qkv(x):
                kvs = []
                qs = []
                for h in range(2):
                    q = dot_t(x, wq[h, l])
                    q = q * lax.rsqrt(jnp.sum(q * q, axis=-1, keepdims=True) * (1.0 / 64.0) + EPS_UNIT)
                    qs.append(q.astype(BF16))
                    kv = dot_t(x, wkv[h, l])
                    kq = jnp.where(lane128 < 64, kv * kv, 0.0)
                    scale = lax.rsqrt(jnp.sum(kq, axis=-1, keepdims=True) * (1.0 / 64.0) + EPS_UNIT)
                    kvs.append((kv * jnp.where(lane128 < 64, scale, 1.0)).astype(BF16))
                return qs, kvs

            qs, kvs = gather_rows(layer_norm(resid[...], gains[l, pl.ds(0, 1), :]), qkv)
            kvo[0] = kvs[0]
            kvo[1] = kvs[1]
            cs = []
            for k in range(7):
                for j in range(2):
                    cs.append(remote(kvo.at[j], kvb.at[l, s, i], s_kv_s.at[2 * k + j],
                                     s_kv_r.at[l, 2 * k + i], (seq_dst[k], p * 2 + j)))
            for c in cs:
                c.start()
            qx[0] = qs[0]
            qx[1] = qs[1]
            cq = partner(qx.at[1 - i], qb.at[i], 1)
            cq.start()
            ck = partner(kvo.at[1 - i], kvb.at[l, s, i], 2)
            ck.start()
            qb[i] = qx[i]
            kvb[l, s, i] = kvo[i]
            partner(qx.at[1 - i], qb.at[1 - i], 1).wait_recv()
            partner(kvo.at[1 - i], kvb.at[l, s, 1 - i], 2).wait_recv()
            scale = temp[l, 0] * (1.0 / 64.0)
            q = qb[...].reshape(256, 128)
            num = jnp.zeros((256, 128), F32)
            den = jnp.zeros((256, 128), F32)
            for k in (7, 6, 5, 4, 3, 2, 1, 0):
                if k == 7:
                    src = s
                else:
                    src = seq_src[k]
                    for j in range(2):
                        remote(kvo.at[j], kvb.at[l, src, j], s_kv_s.at[2 * k + j],
                               s_kv_r.at[l, 2 * k + j], (seq_dst[k], p * 2 + j)).wait_recv()
                kv = kvb[l, src].reshape(256, 128)
                e = jnp.exp(dot_t(q, kv) * scale)
                den = den + e[:, :128] + e[:, 128:]
                num = num + dot(e.astype(BF16), kv)
            att = (num / jnp.sum(den, axis=-1, keepdims=True)).astype(BF16)
            ax[...] = att.reshape(2, 128, 128)
            ca = partner(ax.at[1 - i], ab, 3)
            ca.start()
            part = dot(ax[i], wo[i, l])
            ca.wait_recv()
            part = part + dot(ab[...], wo[1 - i, l])
            for c in cs:
                c.wait_send()
            cq.wait_send()
            ck.wait_send()
            ca.wait_send()
            sum_rows(part)

            def ffn(x):
                part = jnp.zeros((128, 1024), F32)
                for h in range(2):
                    hid = dot(x, wu[h, l])
                    hid = 0.5 * hid * (1.0 + lax.erf(hid * (0.5 ** 0.5)))
                    part = part + dot(hid.astype(BF16), wd[h, l])
                return part

            sum_rows(gather_rows(layer_norm(resid[...], gains[l, pl.ds(1, 1), :]), ffn))
            return carry

        lax.fori_loop(0, LAYERS, layer_body, 0)
        fb[i] = layer_norm(resid[...], fgain[...]).astype(BF16)
        c = partner(fb.at[i], fb.at[i], 4)
        c.start()
        partner(fb.at[i], fb.at[1 - i], 4).wait_recv()
        fin = fb[...].reshape(32, 1024)
        for q in range(8):
            d = dot_t(fin, headp[q])
            st[q] = st[q] + d
            db[step, q] = d.astype(BF16)
        c.wait_send()
        for k in range(7):
            remote(db.at[step, var_dst[k]], dlr.at[step, p], s_d_s.at[step, k], s_d_r.at[step, k],
                   var_dev(var_dst[k])).start()
        dlr[step, p] = db[step, p]
        return carry

    lax.fori_loop(0, STEPS, step_body, 0)

    state = fields[...]
    for step in range(STEPS):
        for k in range(7):
            c = remote(db.at[step, var_dst[k]], dlr.at[step, var_src[k]], s_d_s.at[step, k],
                       s_d_r.at[step, k], var_dev(var_dst[k]))
            c.wait_recv()
            c.wait_send()
        d = jnp.transpose(dlr[step].astype(F32).reshape(256, 128))
        state = state + d[:48]
        out[step] = state


def per_device(
    fields, channel_ids, lead_index, embed_weight, var_table, agg_query, agg_kv, agg_out,
    agg_temp, pos_table, lead_table, norm_gain, qkv_weight, attn_temp, out_weight,
    up_weight, down_weight, final_gain, head_weight,
):
    vm = pl.BlockSpec(memory_space=pltpu.VMEM)
    sm = pl.BlockSpec(memory_space=pltpu.SMEM)
    hb = pl.BlockSpec(memory_space=pl.ANY)
    dma = pltpu.SemaphoreType.DMA
    V = pltpu.VMEM
    qkv_t = jnp.transpose(qkv_weight, (0, 2, 3, 1)).reshape(LAYERS, 192, 1024)
    head_t = jnp.transpose(head_weight, (1, 2, 0)).reshape(8, 2, 48, 1024)
    out = pl.pallas_call(
        kernel,
        out_shape=jax.ShapeDtypeStruct((STEPS, 48, 256), F32),
        in_specs=[vm, sm, sm, hb, vm, vm, hb, hb, vm, hb, vm, vm, hb, sm, hb, hb, hb, vm, hb],
        out_specs=vm,
        scratch_shapes=[
            V((2, LAYERS, 128, 1024), BF16),
            V((2, LAYERS, 128, 1024), BF16),
            V((2, LAYERS, 128, 1024), BF16),
            V((2, LAYERS, 1024, 256), BF16),
            V((2, LAYERS, 256, 1024), BF16),
            V((1024, 2048), BF16),
            V((1024, 1024), BF16),
            V((8, 128, 1024), BF16),
            V((16, 1024), BF16),
            V((8, 32, 128), F32),
            V((8, 32, 128), F32),
            V((8, 48, 1024), BF16),
            V((8, 8, 1024), BF16),
            V((8, 1024), BF16),
            V((8, 48, 2048), BF16),
            V((8, 8, 2048), F32),
            V((8, 96, 1024), BF16),
            V((8, 96, 1024), BF16),
            V((8, 96, 1024), F32),
            V((8, 96, 128), BF16),
            V((32, 2048), F32),
            V((2, 16, 2048), F32),
            V((16, 2048), F32),
            V((128, 1024), BF16),
            V((128, 1024), BF16),
            V((16, 1024), F32),
            V((8, 16, 1024), BF16),
            V((8, 16, 1024), BF16),
            V((7, 16, 1024), BF16),
            V((2, 128, 128), BF16),
            V((2, 128, 128), BF16),
            V((LAYERS, 8, 2, 128, 128), BF16),
            V((2, 128, 128), BF16),
            V((2, 128, 128), BF16),
            V((128, 128), BF16),
            V((2, 16, 1024), BF16),
            V((STEPS, 8, 32, 128), BF16),
            V((STEPS, 8, 32, 128), BF16),
            dma((10,)),
            dma((5,)), dma((5,)),
            dma((7,)), dma((7,)),
            dma((7,)), dma((7,)),
            dma((7,)), dma((7,)),
            dma((7,)), dma((7,)),
            dma((7,)), dma((7,)),
            dma((14,)), dma((LAYERS, 14)),
            dma((5,)), dma((5,)),
            dma((STEPS, 7)), dma((STEPS, 7)),
        ],
        compiler_params=pltpu.CompilerParams(
            collective_id=0, has_side_effects=True, vmem_limit_bytes=60 * 1024 * 1024
        ),
        name="rollout",
    )(
        fields.reshape(48, 256),
        channel_ids,
        lead_index,
        embed_weight.reshape(48, 1024),
        var_table,
        agg_query,
        agg_kv.reshape(1024, 2048),
        agg_out,
        agg_temp.reshape(1, 16),
        pos_table,
        lead_table,
        norm_gain,
        qkv_t,
        attn_temp,
        out_weight.reshape(LAYERS, 64, 1024),
        up_weight,
        down_weight,
        final_gain.reshape(1, 1024),
        head_t,
    )
    return out.reshape(STEPS, 3, 16, 1, 256)


def solution(mesh):
    return jax.shard_map(
        per_device,
        mesh=mesh,
        in_specs=(
            P("var", None, None, "seq"),
            P("var"),
            P(),
            P("var", None, None),
            P(),
            P(),
            P(),
            P(),
            P(),
            P("seq", None),
            P(),
            P(),
            P(None, None, "var", None),
            P(None, "var"),
            P(None, "var", None, None),
            P(None, None, "var"),
            P(None, "var", None),
            P(),
            P(),
        ),
        out_specs=P(None, "var", None, None, "seq"),
        check_vma=False,
    )
```

time: 611 us -> 186 us (0.30)
  blocking collectives: 288 us -> 0 us
  Pallas kernels: 0 us -> 175 us
  waiting for transfers between devices: 165 us -> 0 us
  matrix products: 46.8 us -> 0 us
  other arithmetic: 35.6 us -> 0 us
  starting transfers between devices: 26.1 us -> 0 us
  local copies, waits for them, and re-layouts: 31.1 us -> 9.87 us
  between operations: 16.1 us -> 0.66 us
    all_to_all x17 -> x0, blocking collectives: 288 us -> none  [the longest x8 161 us: sent_and_summed(): lax.all_to_all(pieces, axis, split_axis=0, concat_axis=0, tiled=True)]
    pallas_call x0 -> x1, Pallas kernels: none -> 175 us  [per_device(): pl.pallas_call(kernel, out_shape=jax.ShapeDtypeStruct((STEPS, 48, 256), F...]
    reduce_scatter x2 -> x0, waiting for transfers between devices: 119 us -> none  [side_by_side(): lax.psum_scatter(both, axis, scatter_dimension=dim, tiled=True)]
    dot_general x33 -> x0, matrix products: 46.8 us -> none  [the longest x2 17.6 us: per_device(): jnp.dot(tokens.reshape(local_vars * local_rows, width), kv_mat, preferred...]
    all_to_all x5 -> x0, waiting for transfers between devices: 46.1 us -> none  [from_everyone(): lax.all_to_all(jnp.broadcast_to(shard[None], (count, *shard.shape)), axis...]
    reduce_sum x39 -> x0, other arithmetic: 28.2 us -> none  [the longest x8 8.51 us: sent_and_summed(): return arrived.sum(axis=0)]
    all_to_all x5 -> x0, starting transfers between devices: 26.1 us -> none  [from_everyone(): lax.all_to_all(jnp.broadcast_to(shard[None], (count, *shard.shape)), axis...]
    broadcast_in_dim x18 -> x0, local copies, waits for them, and re-layouts: 6.91 us -> none  [from_everyone(): jnp.broadcast_to(shard[None], (count, *shard.shape))]
  transfers between devices with their start and end apart: 7 -> 0, of which waited for: 7 -> 0; matrix products, arithmetic and copies ran while one was open for 1% -> 0% of each run, Pallas kernels for 0% -> 0%
where the time goes in v1:
time: 186 us
  Pallas kernels  175 us (94%)
  local copies, waits for them, and re-layouts  9.87 us (5%)
    pallas_call x1, Pallas kernels, per_device(): pl.pallas_call(kernel, out_shape=jax.ShapeDtypeStruct((STEPS, 48, 256), F...  175 us
    unnamed x3, local copies, waits for them, and re-layouts  8.24 us

profile of v1, /device:TPU:1, one launch (start us, length us, event | category | flops | bytes accessed | tf_op | source)
XLA Modules:
  0.0 185.6 jit_solution(3215926112882042355)
XLA Ops:
  0.7 1.3 copy.21.temp
  1.9 1.4 copy.23
  3.4 5.5 %copy.24 = bf16[128,8,2,1024]{3,1,2,0:T(8,128)(2,1)} copy(bf16[128,8,2,1024]{3,2,1,0:T(2,128)(2,1)} %bitcast.17) | data formatting | bytes 8388608
  8.9 175.1 %rollout.1 = f32[2,48,256]{2,1,0:T(8,128)} custom-call(f32[48,256]{1,0:T(8,128)} %bitcast.22, s32[3]{0:T(128)} %ids.1, s32[1]{0:T(128)S(6)} %copy.25.lead, bf16[48,1024]{1,0:T(8,128)(2,1)} %bitcast.23, bf16[48,1024]{1,0:T(8,128)(2,1)} %vart.1, bf16[16,64]{1,0:T(8,128)(2,1)} %aquery.1, bf16[1024,2048]{1,0:T(8,128)(2,1)} %bitcast.16, ...), custom_call_target="tpu_custom_call" | custom-call | tf_op jit(solution)/shard_map/rollout/pallas_call | solution.py:349
  184.0 1.6 copy.22

commit v2 on v1

--- a/solution.py
+++ b/solution.py
@@ -32,13 +32,14 @@
 
 
 def kernel(
-    fields, ids, lead, emb, vart, aquery, kv_h, aout_h, atemp, pos_h, leadt, gains,
-    qkv_h, temp, wo_h, up_h, dn_h, fgain, head_h,
+    ids, lead, temp, fields_h, emb, vart_h, aquery_h, kv_h, aout_h, atemp_h, pos_h, leadt_h, gains_h,
+    qkv_h, wo_h, up_h, dn_h, fgain_h, head_h,
     out,
+    fields, vart, aquery, atemp, leadt, gains, fgain, kv3,
     wq, wkv, wo, wu, wd, kvv, aout, headp, posv,
-    fsnd, st, we, vr, vrt, mb, bb, kb, k2, vv, wb, nd, ndx, ndr, hexp, qexp,
+    fsnd, st, we, mb, kb, k2, vv, wb, ndx, ndr, hexp, qexp,
     resid, xg, pb, rsb, qb, qx, kvb, kvo, ax, ab, fb, db, dlr,
-    s_loc, s_ws, s_wr, s_is, s_ir, s_es, s_er, s_vs, s_vr, s_ag_s, s_ag_r, s_rs_s, s_rs_r,
+    s_loc, s_ws, s_wr, s_is, s_ir, s_es, s_er, s_ag_s, s_ag_r, s_rs_s, s_rs_r,
     s_kv_s, s_kv_r, s_px_s, s_px_r, s_d_s, s_d_r,
 ):
     s = lax.axis_index("seq")
@@ -75,14 +76,14 @@
                  (wo_h, wo.at[i, :, pl.ds(64, 64)]),
                  (up_h, wu.at[i]),
                  (dn_h, wd.at[i]))
-    loads = [pltpu.make_async_copy(kv_h, kvv, s_loc.at[0]),
-             pltpu.make_async_copy(emb, we.at[p], s_loc.at[1]),
-             pltpu.make_async_copy(aout_h, aout, s_loc.at[2]),
-             pltpu.make_async_copy(pos_h.at[pl.ds(v * 16, 16)], posv, s_loc.at[3]),
-             pltpu.make_async_copy(head_h.at[:, i], headp.at[:, pl.ds(0, 48)], s_loc.at[4])]
-    for k, (a, b) in enumerate(own_heads):
-        loads.append(pltpu.make_async_copy(a, b, s_loc.at[5 + k]))
-    for c in loads:
+    loads = []
+    for k, (a, b) in enumerate((
+        (fields_h, fields), (kv_h, kv3), (emb, we.at[p]), (aquery_h, aquery), (vart_h, vart), (atemp_h, atemp),
+        (aout_h, aout), (pos_h.at[pl.ds(v * 16, 16)], posv), (leadt_h, leadt), (gains_h, gains),
+        (fgain_h, fgain), (head_h.at[:, i], headp.at[:, pl.ds(0, 48)]), *own_heads,
+    )):
+        loads.append(pltpu.make_async_copy(a, b, s_loc.at[k]))
+    for c in loads[:6]:
         c.start()
 
     bar = pltpu.get_barrier_semaphore()
@@ -93,21 +94,21 @@
             pl.semaphore_signal(bar, inc=1, device_id=(t, p * 2 + j), device_id_type=MESH)
     pl.semaphore_signal(bar, inc=1, device_id=other, device_id_type=MESH)
 
-    lane16 = lax.broadcasted_iota(jnp.int32, (32, 48), 1) // 16
-    fpad = jnp.concatenate([fields[...], jnp.zeros((80, 256), F32)], axis=0)
-    fsnd[...] = jnp.transpose(fpad).reshape(8, 32, 128)
-    row8 = lax.broadcasted_iota(jnp.int32, (8, 48), 0)
-    ch8 = lax.broadcasted_iota(jnp.int32, (8, 48), 1)
-    named = jnp.where(row8 == 0, ids[0], jnp.where(row8 == 1, ids[1], ids[2]))
-    hot = jnp.where((named == ch8) & (row8 < 3), 1.0, 0.0).astype(BF16)
-    vrt[...] = dot(hot, vart[...]).astype(BF16)
+    for c in loads[6:]:
+        c.start()
+    loads[0].wait()
+    state0 = fields[:, 0, :]
+    frow = lax.broadcasted_iota(jnp.int32, (80, 256), 0)
+    fcol = lax.broadcasted_iota(jnp.int32, (80, 256), 1) % 32
+    named = jnp.where(fcol == 0, ids[0], jnp.where(fcol == 1, ids[1], jnp.where(fcol == 2, ids[2], 0)))
+    extra = jnp.where(frow == 0, named, 0).astype(F32)
+    fsnd[...] = jnp.transpose(jnp.concatenate([state0, extra], axis=0)).reshape(8, 32, 128)
 
     pl.semaphore_wait(bar, 22)
 
     init = []
     for k in range(7):
         init.append(remote(fsnd.at[var_dst[k]], st.at[p], s_is.at[k], s_ir.at[k], var_dev(var_dst[k])))
-        init.append(remote(vrt, vr.at[p], s_vs.at[k], s_vr.at[k], var_dev(var_dst[k])))
         init.append(remote(emb, we.at[p], s_es.at[k], s_er.at[k], var_dev(var_dst[k])))
     for c in init:
         c.start()
@@ -118,7 +119,6 @@
         c.start()
 
     st[p] = fsnd[p]
-    vr[p] = vrt[...]
     wq[:, :, pl.ds(64, 64)] = jnp.zeros((2, LAYERS, 64, 1024), BF16)
     wo[:, :, pl.ds(0, 64)] = jnp.zeros((2, LAYERS, 64, 1024), BF16)
     headp[:, pl.ds(48, 80)] = jnp.zeros((8, 80, 1024), BF16)
@@ -126,48 +126,60 @@
     hrow = lax.broadcasted_iota(jnp.int32, (128, 1024), 0)
     hcol = lax.broadcasted_iota(jnp.int32, (128, 1024), 1) // 64
     hexp[...] = jnp.where(hrow == hcol, 1.0, 0.0).astype(BF16)
+    loads[3].wait()
     aq = aquery[...].astype(F32)
     aq = aq * lax.rsqrt(jnp.mean(aq * aq, axis=-1, keepdims=True) + EPS_UNIT)
     aqt = jnp.concatenate([aq] * 16, axis=1)
     aqt = jnp.concatenate([aqt, jnp.zeros((112, 1024), F32)], axis=0)
     qexp[...] = jnp.where(hrow == hcol, aqt, 0.0).astype(BF16)
+    for c in loads[4:6]:
+        c.wait()
     tvec = jnp.concatenate([atemp[...] * (1.0 / 64.0), jnp.zeros((1, 112), F32)], axis=1)
 
-    loads[0].wait()
     loads[1].wait()
+
+    def split_kv(n, c):
+        rows = pl.ds(n * 64, 64)
+        kvv[rows] = kv3[rows].reshape(64, 2048)
+        return c
+
+    lax.fori_loop(0, 16, split_kv, 0)
+    loads[2].wait()
+    for k in range(7):
+        remote(fsnd.at[0], st.at[var_src[k]], s_is.at[k], s_ir.at[k], var_dev(var_dst[k])).wait_recv()
+    nrow = lax.broadcasted_iota(jnp.int32, (128, 48), 0) % 16
+    ncol = lax.broadcasted_iota(jnp.int32, (128, 48), 1).astype(F32)
+    named = st[:, pl.ds(0, 16)].reshape(128, 128)[:, 48:49]
+    hot = jnp.where((named == ncol) & (nrow < 3), 1.0, 0.0).astype(BF16)
+    vall = dot(hot, vart[...]).astype(BF16)
+    for n in range(4):
+        cols = pl.ds(n * 512, 512)
+        mb[:, pl.ds(48, 16), cols] = dot(vall, kvv[:, cols]).astype(BF16).reshape(8, 16, 512)
     for k in range(7):
         remote(emb, we.at[var_src[k]], s_es.at[k], s_er.at[k], var_dev(var_dst[k])).wait_recv()
-        remote(vrt, vr.at[var_src[k]], s_vs.at[k], s_vr.at[k], var_dev(var_dst[k])).wait_recv()
-
     wall = we[...].reshape(384, 1024)
-    vall = vr[...].reshape(64, 1024)
     for n in range(4):
         cols = pl.ds(n * 512, 512)
-        mb[:, :, cols] = dot(wall, kvv[:, cols]).astype(BF16).reshape(8, 48, 512)
-        bb[:, :, cols] = dot(vall, kvv[:, cols]).reshape(8, 8, 512)
-    for k in range(7):
-        remote(fsnd.at[0], st.at[var_src[k]], s_is.at[k], s_ir.at[k], var_dev(var_dst[k])).wait_recv()
+        mb[:, pl.ds(0, 48), cols] = dot(wall, kvv[:, cols]).astype(BF16).reshape(8, 48, 512)
     for c in init:
         c.wait_send()
-    for c in loads[2:5]:
+    for c in loads[6:12]:
         c.wait()
 
+    lane64 = lax.broadcasted_iota(jnp.int32, (32, 64), 1)
     lane128 = lax.broadcasted_iota(jnp.int32, (128, 128), 1)
 
     def partner(src, dst, k):
         return remote(src, dst, s_px_s.at[k], s_px_r.at[k], other)
 
-    def gather_rows(normed, work):
+    def gather_rows(normed):
         xg[p] = normed.astype(BF16)
         cs = [remote(xg.at[p], xg.at[p], s_ag_s.at[k], s_ag_r.at[k], var_dev(var_dst[k])) for k in range(7)]
         for c in cs:
             c.start()
         for k in range(7):
             remote(xg.at[p], xg.at[var_src[k]], s_ag_s.at[k], s_ag_r.at[k], var_dev(var_dst[k])).wait_recv()
-        res = work(xg[...].reshape(128, 1024))
-        for c in cs:
-            c.wait_send()
-        return res
+        return xg[...].reshape(128, 1024), cs
 
     def sum_rows(part):
         pb[...] = part.astype(BF16).reshape(8, 16, 1024)
@@ -183,33 +195,28 @@
             c.wait_send()
 
     def step_body(step, carry):
-        def pool_keys(q, c):
-            sb = st[q][:, :48]
-            blk = jnp.concatenate([jnp.where(lane16 == n, sb, 0.0) for n in range(3)], axis=0).astype(BF16)
-            bias = bb[q]
-            brow = jnp.concatenate([jnp.broadcast_to(bias[n:n + 1], (32, 2048)) for n in range(3)], axis=0)
-            kk = dot(blk, mb[q, :, pl.ds(0, 1024)]) + brow[:, :1024]
+        for q in range(8):
+            sb = st[q][:, :64]
+            blk = jnp.concatenate(
+                [jnp.where(lane64 // 16 == n, sb, jnp.where(lane64 == 48 + n, 1.0, 0.0)) for n in range(3)], axis=0
+            ).astype(BF16)
+            kk = dot(blk, mb[q, :, pl.ds(0, 1024)])
             kb[q] = kk.astype(BF16)
             k2[q] = (kk * kk).astype(BF16)
-            vv[q] = dot(blk, mb[q, :, pl.ds(1024, 1024)]) + brow[:, 1024:]
-            return c
-
-        lax.fori_loop(0, 8, pool_keys, 0)
+            vv[q] = dot(blk, mb[q, :, pl.ds(1024, 1024)]).astype(BF16)
         ss = dot_t(k2[...].reshape(768, 1024), hexp[...])
         qk = dot_t(kb[...].reshape(768, 1024), qexp[...])
         w = jnp.exp(qk * lax.rsqrt(ss * (1.0 / 64.0) + EPS_UNIT) * tvec)
         wb[...] = w.astype(BF16).reshape(8, 96, 128)
-        nd[...] = jnp.zeros((32, 2048), F32)
-
-        def pool_sum(q, c):
+        num = jnp.zeros((32, 1024), F32)
+        den = jnp.zeros((32, 1024), F32)
+        for q in range(8):
             wx = dot(wb[q], hexp[...])
-            num = wx * vv[q]
-            nd[:, pl.ds(0, 1024)] = nd[:, pl.ds(0, 1024)] + (num[0:32] + num[32:64] + num[64:96])
-            nd[:, pl.ds(1024, 1024)] = nd[:, pl.ds(1024, 1024)] + (wx[0:32] + wx[32:64] + wx[64:96])
-            return c
-
-        lax.fori_loop(0, 8, pool_sum, 0)
-        ndx[...] = nd[...].reshape(2, 16, 2048)
+            nx = wx * vv[q].astype(F32)
+            num = num + (nx[0:32] + nx[32:64] + nx[64:96])
+            den = den + (wx[0:32] + wx[32:64] + wx[64:96])
+        ndx[:, :, pl.ds(0, 1024)] = num.reshape(2, 16, 1024)
+        ndx[:, :, pl.ds(1024, 1024)] = den.reshape(2, 16, 1024)
         c = partner(ndx.at[1 - i], ndr, 0)
         c.start()
         row16 = lax.broadcasted_iota(jnp.int32, (16, 16), 1)
@@ -223,46 +230,39 @@
 
         @pl.when(step == 0)
         def _():
-            for c in loads[5:]:
+            for c in loads[12:]:
                 c.wait()
             for c in wcopies:
                 c.wait()
 
         def layer_body(l, carry):
-            def qkv(x):
-                kvs = []
-                qs = []
-                for h in range(2):
-                    q = dot_t(x, wq[h, l])
-                    q = q * lax.rsqrt(jnp.sum(q * q, axis=-1, keepdims=True) * (1.0 / 64.0) + EPS_UNIT)
-                    qs.append(q.astype(BF16))
-                    kv = dot_t(x, wkv[h, l])
-                    kq = jnp.where(lane128 < 64, kv * kv, 0.0)
-                    scale = lax.rsqrt(jnp.sum(kq, axis=-1, keepdims=True) * (1.0 / 64.0) + EPS_UNIT)
-                    kvs.append((kv * jnp.where(lane128 < 64, scale, 1.0)).astype(BF16))
-                return qs, kvs
-
-            qs, kvs = gather_rows(layer_norm(resid[...], gains[l, pl.ds(0, 1), :]), qkv)
-            kvo[0] = kvs[0]
-            kvo[1] = kvs[1]
+            x, cg = gather_rows(layer_norm(resid[...], gains[l, pl.ds(0, 1), :]))
             cs = []
-            for k in range(7):
-                for j in range(2):
-                    cs.append(remote(kvo.at[j], kvb.at[l, s, i], s_kv_s.at[2 * k + j],
-                                     s_kv_r.at[l, 2 * k + i], (seq_dst[k], p * 2 + j)))
-            for c in cs:
-                c.start()
-            qx[0] = qs[0]
-            qx[1] = qs[1]
+            for h in range(2):
+                kv = dot_t(x, wkv[h, l])
+                kq = jnp.where(lane128 < 64, kv * kv, 0.0)
+                scale = lax.rsqrt(jnp.sum(kq, axis=-1, keepdims=True) * (1.0 / 64.0) + EPS_UNIT)
+                kvo[h] = (kv * jnp.where(lane128 < 64, scale, 1.0)).astype(BF16)
+                for k in range(7):
+                    c = remote(kvo.at[h], kvb.at[l, s, i], s_kv_s.at[2 * k + h],
+                               s_kv_r.at[l, 2 * k + i], (seq_dst[k], p * 2 + h))
+                    c.start()
+                    cs.append(c)
+            ck = partner(kvo.at[1 - i], kvb.at[l, s, i], 2)
+            ck.start()
+            for h in range(2):
+                q = dot_t(x, wq[h, l])
+                q = q * lax.rsqrt(jnp.sum(q * q, axis=-1, keepdims=True) * (1.0 / 64.0) + EPS_UNIT)
+                qx[h] = q.astype(BF16)
             cq = partner(qx.at[1 - i], qb.at[i], 1)
             cq.start()
-            ck = partner(kvo.at[1 - i], kvb.at[l, s, i], 2)
-            ck.start()
             qb[i] = qx[i]
             kvb[l, s, i] = kvo[i]
+            for c in cg:
+                c.wait_send()
             partner(qx.at[1 - i], qb.at[1 - i], 1).wait_recv()
             partner(kvo.at[1 - i], kvb.at[l, s, 1 - i], 2).wait_recv()
-            scale = temp[l, 0] * (1.0 / 64.0)
+            scale = temp[l] * (1.0 / 64.0)
             q = qb[...].reshape(256, 128)
             num = jnp.zeros((256, 128), F32)
             den = jnp.zeros((256, 128), F32)
@@ -292,15 +292,15 @@
             ca.wait_send()
             sum_rows(part)
 
-            def ffn(x):
-                part = jnp.zeros((128, 1024), F32)
-                for h in range(2):
-                    hid = dot(x, wu[h, l])
-                    hid = 0.5 * hid * (1.0 + lax.erf(hid * (0.5 ** 0.5)))
-                    part = part + dot(hid.astype(BF16), wd[h, l])
-                return part
-
-            sum_rows(gather_rows(layer_norm(resid[...], gains[l, pl.ds(1, 1), :]), ffn))
+            x, cg = gather_rows(layer_norm(resid[...], gains[l, pl.ds(1, 1), :]))
+            part = jnp.zeros((128, 1024), F32)
+            for h in range(2):
+                hid = dot(x, wu[h, l])
+                hid = 0.5 * hid * (1.0 + lax.erf(hid * (0.5 ** 0.5)))
+                part = part + dot(hid.astype(BF16), wd[h, l])
+            for c in cg:
+                c.wait_send()
+            sum_rows(part)
             return carry
 
         lax.fori_loop(0, LAYERS, layer_body, 0)
@@ -322,7 +322,7 @@
 
     lax.fori_loop(0, STEPS, step_body, 0)
 
-    state = fields[...]
+    state = fields[:, 0, :]
     for step in range(STEPS):
         for k in range(7):
             c = remote(db.at[step, var_dst[k]], dlr.at[step, var_src[k]], s_d_s.at[step, k],
@@ -331,7 +331,7 @@
             c.wait_send()
         d = jnp.transpose(dlr[step].astype(F32).reshape(256, 128))
         state = state + d[:48]
-        out[step] = state
+        out[step] = state.reshape(48, 1, 256)
 
 
 def per_device(
@@ -348,10 +348,18 @@
     head_t = jnp.transpose(head_weight, (1, 2, 0)).reshape(8, 2, 48, 1024)
     out = pl.pallas_call(
         kernel,
-        out_shape=jax.ShapeDtypeStruct((STEPS, 48, 256), F32),
-        in_specs=[vm, sm, sm, hb, vm, vm, hb, hb, vm, hb, vm, vm, hb, sm, hb, hb, hb, vm, hb],
+        out_shape=jax.ShapeDtypeStruct((STEPS, 48, 1, 256), F32),
+        in_specs=[sm] * 3 + [hb] * 16,
         out_specs=vm,
         scratch_shapes=[
+            V((48, 1, 256), F32),
+            V((48, 1024), BF16),
+            V((16, 64), BF16),
+            V((1, 16), F32),
+            V((16, 1024), BF16),
+            V((LAYERS, 2, 1024), F32),
+            V((1, 1024), F32),
+            V((1024, 2, 1024), BF16),
             V((2, LAYERS, 128, 1024), BF16),
             V((2, LAYERS, 128, 1024), BF16),
             V((2, LAYERS, 128, 1024), BF16),
@@ -364,15 +372,11 @@
             V((8, 32, 128), F32),
             V((8, 32, 128), F32),
             V((8, 48, 1024), BF16),
-            V((8, 8, 1024), BF16),
-            V((8, 1024), BF16),
-            V((8, 48, 2048), BF16),
-            V((8, 8, 2048), F32),
+            V((8, 64, 2048), BF16),
             V((8, 96, 1024), BF16),
             V((8, 96, 1024), BF16),
-            V((8, 96, 1024), F32),
+            V((8, 96, 1024), BF16),
             V((8, 96, 128), BF16),
-            V((32, 2048), F32),
             V((2, 16, 2048), F32),
             V((16, 2048), F32),
             V((128, 1024), BF16),
@@ -390,9 +394,8 @@
             V((2, 16, 1024), BF16),
             V((STEPS, 8, 32, 128), BF16),
             V((STEPS, 8, 32, 128), BF16),
-            dma((10,)),
+            dma((17,)),
             dma((5,)), dma((5,)),
-            dma((7,)), dma((7,)),
             dma((7,)), dma((7,)),
             dma((7,)), dma((7,)),
             dma((7,)), dma((7,)),
@@ -406,20 +409,20 @@
         ),
         name="rollout",
     )(
-        fields.reshape(48, 256),
         channel_ids,
         lead_index,
+        attn_temp.reshape(LAYERS),
+        fields.reshape(48, 1, 256),
         embed_weight.reshape(48, 1024),
         var_table,
         agg_query,
-        agg_kv.reshape(1024, 2048),
+        agg_kv,
         agg_out,
         agg_temp.reshape(1, 16),
         pos_table,
         lead_table,
         norm_gain,
         qkv_t,
-        attn_temp,
         out_weight.reshape(LAYERS, 64, 1024),
         up_weight,
         down_weight,

time: 186 us -> 166 us (0.89)
  Pallas kernels: 175 us -> 164 us
  local copies, waits for them, and re-layouts: 9.87 us -> 1.54 us
    pallas_call x1, Pallas kernels: 175 us -> 164 us  [per_device(): pl.pallas_call(kernel, out_shape=jax.ShapeDtypeStruct((STEPS, 48, 1, 256)...]
    unnamed x3 -> x1, local copies, waits for them, and re-layouts: 8.24 us -> 1.54 us
where the time goes in v2:
time: 166 us
  Pallas kernels  164 us (99%)
    pallas_call x1, Pallas kernels, per_device(): pl.pallas_call(kernel, out_shape=jax.ShapeDtypeStruct((STEPS, 48, 1, 256)...  164 us

profile of v2, /device:TPU:1, one launch (start us, length us, event | category | flops | bytes accessed | tf_op | source)
XLA Modules:
  0.0 165.8 jit_solution(16424516795952541377)
XLA Ops:
  0.7 163.6 %rollout.1 = f32[2,48,1,256]{3,2,1,0:T(1,128)} custom-call(s32[3]{0:T(128)} %ids.1, s32[1]{0:T(128)S(6)} %copy.22.lead, f32[2]{0:T(128)} %bitcast.22, f32[48,1,256]{2,1,0:T(1,128)} %bitcast.20, bf16[48,1024]{1,0:T(8,128)(2,1)} %bitcast.19, bf16[48,1024]{1,0:T(8,128)(2,1)} %vart_h.1, bf16[16,64]{1,0:T(8,128)(2,1)} %aquery_h.1, bf16[1024,2,1024]{2,1,0:T(2,128)(2,1)} %kv_h.1, ...), custom_call_target="tpu_custom_call" | custom-call | tf_op jit(solution)/shard_map/rollout/pallas_call | solution.py:349
  164.3 1.5 copy.23

commit v3 on v2

--- a/solution.py
+++ b/solution.py
@@ -38,9 +38,10 @@
     fields, vart, aquery, atemp, leadt, gains, fgain, kv3,
     wq, wkv, wo, wu, wd, kvv, aout, headp, posv,
     fsnd, st, we, mb, kb, k2, vv, wb, ndx, ndr, hexp, qexp,
-    resid, xg, pb, rsb, qb, qx, kvb, kvo, ax, ab, fb, db, dlr,
+    resid, xg, pb, rsb, qb, qx, kvb, kvo, ax, ab, at, rs, fb, db, dlr,
     s_loc, s_ws, s_wr, s_is, s_ir, s_es, s_er, s_ag_s, s_ag_r, s_rs_s, s_rs_r,
     s_kv_s, s_kv_r, s_px_s, s_px_r, s_d_s, s_d_r,
+    s_at_s, s_at_r, s_wo_s, s_wo_r, s_wp_s, s_wp_r,
 ):
     s = lax.axis_index("seq")
     v = lax.axis_index("var")
@@ -73,14 +74,13 @@
 
     own_heads = ((qkv_h.at[:, pl.ds(0, 64)], wq.at[i, :, pl.ds(0, 64)]),
                  (qkv_h.at[:, pl.ds(64, 128)], wkv.at[i]),
-                 (wo_h, wo.at[i, :, pl.ds(64, 64)]),
                  (up_h, wu.at[i]),
                  (dn_h, wd.at[i]))
     loads = []
     for k, (a, b) in enumerate((
         (fields_h, fields), (kv_h, kv3), (emb, we.at[p]), (aquery_h, aquery), (vart_h, vart), (atemp_h, atemp),
         (aout_h, aout), (pos_h.at[pl.ds(v * 16, 16)], posv), (leadt_h, leadt), (gains_h, gains),
-        (fgain_h, fgain), (head_h.at[:, i], headp.at[:, pl.ds(0, 48)]), *own_heads,
+        (fgain_h, fgain), (head_h.at[:, i], headp.at[:, pl.ds(0, 48)]), *own_heads, (wo_h, wo.at[:, v]),
     )):
         loads.append(pltpu.make_async_copy(a, b, s_loc.at[k]))
     for c in loads[:6]:
@@ -88,7 +88,8 @@
 
     bar = pltpu.get_barrier_semaphore()
     for q in var_dst:
-        pl.semaphore_signal(bar, inc=1, device_id=var_dev(q), device_id_type=MESH)
+        for j in range(2):
+            pl.semaphore_signal(bar, inc=1, device_id=(s, q * 2 + j), device_id_type=MESH)
     for t in seq_dst:
         for j in range(2):
             pl.semaphore_signal(bar, inc=1, device_id=(t, p * 2 + j), device_id_type=MESH)
@@ -104,7 +105,7 @@
     extra = jnp.where(frow == 0, named, 0).astype(F32)
     fsnd[...] = jnp.transpose(jnp.concatenate([state0, extra], axis=0)).reshape(8, 32, 128)
 
-    pl.semaphore_wait(bar, 22)
+    pl.semaphore_wait(bar, 29)
 
     init = []
     for k in range(7):
@@ -113,14 +114,31 @@
     for c in init:
         c.start()
     wcopies = []
-    for k, (a, b) in enumerate(own_heads):
+    for k, (a, b) in enumerate((*own_heads, (wo_h, wo.at[:, v]))):
         wcopies.append(remote(a, b, s_ws.at[k], s_wr.at[k], other))
     for c in wcopies:
         c.start()
 
+    def wo_copy(l, k):
+        return remote(wo_h.at[l], wo.at[l, v], s_wo_s.at[l, k], s_wo_r.at[l, k], var_dev(var_dst[k]))
+
+    def wo_arrival(l, k):
+        h = var_src[k] * 2 + i
+        return remote(wo_h.at[l], wo.at[l, h], s_wo_s.at[l, k], s_wo_r.at[l, k], var_dev(var_dst[k]))
+
+    def wo_pass(l, k):
+        h = var_src[k] * 2 + i
+        return remote(wo.at[l, h], wo.at[l, h], s_wp_s.at[l, k], s_wp_r.at[l, k], other)
+
+    def wo_passed(l, k):
+        h = var_src[k] * 2 + 1 - i
+        return remote(wo.at[l, h], wo.at[l, h], s_wp_s.at[l, k], s_wp_r.at[l, k], other)
+
+    for k in range(7):
+        wo_copy(0, k).start()
+
     st[p] = fsnd[p]
     wq[:, :, pl.ds(64, 64)] = jnp.zeros((2, LAYERS, 64, 1024), BF16)
-    wo[:, :, pl.ds(0, 64)] = jnp.zeros((2, LAYERS, 64, 1024), BF16)
     headp[:, pl.ds(48, 80)] = jnp.zeros((8, 80, 1024), BF16)
 
     hrow = lax.broadcasted_iota(jnp.int32, (128, 1024), 0)
@@ -172,8 +190,8 @@
     def partner(src, dst, k):
         return remote(src, dst, s_px_s.at[k], s_px_r.at[k], other)
 
-    def gather_rows(normed):
-        xg[p] = normed.astype(BF16)
+    def gather_rows(own):
+        xg[p] = own.astype(BF16)
         cs = [remote(xg.at[p], xg.at[p], s_ag_s.at[k], s_ag_r.at[k], var_dev(var_dst[k])) for k in range(7)]
         for c in cs:
             c.start()
@@ -186,7 +204,7 @@
         cs = [remote(pb.at[var_dst[k]], rsb.at[k], s_rs_s.at[k], s_rs_r.at[k], var_dev(var_dst[k])) for k in range(7)]
         for c in cs:
             c.start()
-        total = resid[...] + pb[p].astype(F32)
+        total = rs[p] + pb[p].astype(F32)
         for k in (6, 5, 4, 3, 2, 1, 0):
             cs[k].wait_recv()
             total = total + rsb[k].astype(F32)
@@ -232,11 +250,16 @@
         def _():
             for c in loads[12:]:
                 c.wait()
-            for c in wcopies:
+            for c in wcopies[:4]:
                 c.wait()
+            wcopies[4].wait_send()
+            remote(wo_h, wo.at[:, p * 2 + 1 - i], s_ws.at[4], s_wr.at[4], other).wait_recv()
 
         def layer_body(l, carry):
-            x, cg = gather_rows(layer_norm(resid[...], gains[l, pl.ds(0, 1), :]))
+            x, cg = gather_rows(resid[...])
+
+            rows = x.astype(F32)
+            x = layer_norm(rows, gains[l, pl.ds(0, 1), :]).astype(BF16)
             cs = []
             for h in range(2):
                 kv = dot_t(x, wkv[h, l])
@@ -250,6 +273,12 @@
                     cs.append(c)
             ck = partner(kvo.at[1 - i], kvb.at[l, s, i], 2)
             ck.start()
+
+            @pl.when((step == 0) & (l == 0))
+            def _():
+                for k in range(7):
+                    wo_copy(1, k).start()
+
             for h in range(2):
                 q = dot_t(x, wq[h, l])
                 q = q * lax.rsqrt(jnp.sum(q * q, axis=-1, keepdims=True) * (1.0 / 64.0) + EPS_UNIT)
@@ -258,6 +287,13 @@
             cq.start()
             qb[i] = qx[i]
             kvb[l, s, i] = kvo[i]
+
+            @pl.when(step == 0)
+            def _():
+                for k in range(7):
+                    wo_arrival(l, k).wait_recv()
+                    wo_pass(l, k).start()
+
             for c in cg:
                 c.wait_send()
             partner(qx.at[1 - i], qb.at[1 - i], 1).wait_recv()
@@ -278,28 +314,54 @@
                 e = jnp.exp(dot_t(q, kv) * scale)
                 den = den + e[:, :128] + e[:, 128:]
                 num = num + dot(e.astype(BF16), kv)
-            att = (num / jnp.sum(den, axis=-1, keepdims=True)).astype(BF16)
-            ax[...] = att.reshape(2, 128, 128)
-            ca = partner(ax.at[1 - i], ab, 3)
-            ca.start()
-            part = dot(ax[i], wo[i, l])
-            ca.wait_recv()
-            part = part + dot(ab[...], wo[1 - i, l])
+            att = num / jnp.sum(den, axis=-1, keepdims=True)
+            for h in range(2):
+                lo, hi = att[128 * h : 128 * h + 64], att[128 * h + 64 : 128 * h + 128]
+                ax[h] = jnp.where(lane128[:64] < 64, pltpu.roll(lo, 64, 1), hi).astype(BF16)
+            ca = []
+            for k in range(7):
+                for j in range(2):
+                    ca.append(remote(ax.at[j], ab.at[v], s_at_s.at[2 * k + j], s_at_r.at[2 * k + i],
+                                     (s, var_dst[k] * 2 + j)))
+            for c in ca:
+                c.start()
+            cp = partner(ax.at[1 - i], ab.at[v], 3)
+            cp.start()
+            ab[v] = ax[i]
             for c in cs:
                 c.wait_send()
             cq.wait_send()
             ck.wait_send()
-            ca.wait_send()
-            sum_rows(part)
-
-            x, cg = gather_rows(layer_norm(resid[...], gains[l, pl.ds(1, 1), :]))
+
+            @pl.when(step == 0)
+            def _():
+                for k in range(7):
+                    wo_passed(l, k).wait_recv()
+                    wo_pass(l, k).wait_send()
+                    wo_copy(l, k).wait_send()
+
+            partner(ax.at[1 - i], ab.at[p * 2 + 1 - i], 3).wait_recv()
+            for k in range(7):
+                for j in range(2):
+                    remote(ax.at[j], ab.at[var_src[k] * 2 + j], s_at_s.at[2 * k + j], s_at_r.at[2 * k + j],
+                           (s, var_dst[k] * 2 + j)).wait_recv()
+            for q in range(8):
+                even, odd = ab[2 * q].astype(F32), ab[2 * q + 1].astype(F32)
+                cols = pl.ds(q * 128, 128)
+                left = lane128[:64] < 64
+                at[pl.ds(0, 64), cols] = jnp.where(left, even, pltpu.roll(odd, 64, 1)).astype(BF16)
+                at[pl.ds(64, 64), cols] = jnp.where(left, pltpu.roll(even, 64, 1), odd).astype(BF16)
+            rows = rows + dot(at[...], wo[l].reshape(1024, 1024))
+            rs[...] = rows.reshape(8, 16, 1024)
+            x = layer_norm(rows, gains[l, pl.ds(1, 1), :]).astype(BF16)
             part = jnp.zeros((128, 1024), F32)
             for h in range(2):
                 hid = dot(x, wu[h, l])
                 hid = 0.5 * hid * (1.0 + lax.erf(hid * (0.5 ** 0.5)))
                 part = part + dot(hid.astype(BF16), wd[h, l])
-            for c in cg:
+            for c in ca:
                 c.wait_send()
+            cp.wait_send()
             sum_rows(part)
             return carry
 
@@ -362,7 +424,7 @@
             V((1024, 2, 1024), BF16),
             V((2, LAYERS, 128, 1024), BF16),
             V((2, LAYERS, 128, 1024), BF16),
-            V((2, LAYERS, 128, 1024), BF16),
+            V((LAYERS, 16, 64, 1024), BF16),
             V((2, LAYERS, 1024, 256), BF16),
             V((2, LAYERS, 256, 1024), BF16),
             V((1024, 2048), BF16),
@@ -389,8 +451,10 @@
             V((2, 128, 128), BF16),
             V((LAYERS, 8, 2, 128, 128), BF16),
             V((2, 128, 128), BF16),
-            V((2, 128, 128), BF16),
-            V((128, 128), BF16),
+            V((2, 64, 128), BF16),
+            V((16, 64, 128), BF16),
+            V((128, 1024), BF16),
+            V((8, 16, 1024), F32),
             V((2, 16, 1024), BF16),
             V((STEPS, 8, 32, 128), BF16),
             V((STEPS, 8, 32, 128), BF16),
@@ -403,6 +467,9 @@
             dma((14,)), dma((LAYERS, 14)),
             dma((5,)), dma((5,)),
             dma((STEPS, 7)), dma((STEPS, 7)),
+            dma((14,)), dma((14,)),
+            dma((LAYERS, 7)), dma((LAYERS, 7)),
+            dma((LAYERS, 7)), dma((LAYERS, 7)),
         ],
         compiler_params=pltpu.CompilerParams(
             collective_id=0, has_side_effects=True, vmem_limit_bytes=60 * 1024 * 1024

time: 166 us -> 162 us (0.976)
  Pallas kernels: 164 us -> 160 us
    pallas_call x1, Pallas kernels: 164 us -> 160 us  [per_device(): pl.pallas_call(kernel, out_shape=jax.ShapeDtypeStruct((STEPS, 48, 1, 256)...]
where the time goes in v3:
time: 162 us
  Pallas kernels  160 us (99%)
    pallas_call x1, Pallas kernels, per_device(): pl.pallas_call(kernel, out_shape=jax.ShapeDtypeStruct((STEPS, 48, 1, 256)...  160 us

profile of v3, /device:TPU:1, one launch (start us, length us, event | category | flops | bytes accessed | tf_op | source)
XLA Modules:
  0.0 161.9 jit_solution(4526062706620051604)
XLA Ops:
  0.7 159.8 %rollout.1 = f32[2,48,1,256]{3,2,1,0:T(1,128)} custom-call(s32[3]{0:T(128)} %ids.1, s32[1]{0:T(128)S(6)} %copy.22.lead, f32[2]{0:T(128)} %bitcast.22, f32[48,1,256]{2,1,0:T(1,128)} %bitcast.20, bf16[48,1024]{1,0:T(8,128)(2,1)} %bitcast.19, bf16[48,1024]{1,0:T(8,128)(2,1)} %vart_h.1, bf16[16,64]{1,0:T(8,128)(2,1)} %aquery_h.1, bf16[1024,2,1024]{2,1,0:T(2,128)(2,1)} %kv_h.1, ...), custom_call_target="tpu_custom_call" | custom-call | tf_op jit(solution)/shard_map/rollout/pallas_call | solution.py:411
  160.4 1.5 copy.23

commit v4 on v3

--- a/solution.py
+++ b/solution.py
@@ -41,7 +41,7 @@
     resid, xg, pb, rsb, qb, qx, kvb, kvo, ax, ab, at, rs, fb, db, dlr,
     s_loc, s_ws, s_wr, s_is, s_ir, s_es, s_er, s_ag_s, s_ag_r, s_rs_s, s_rs_r,
     s_kv_s, s_kv_r, s_px_s, s_px_r, s_d_s, s_d_r,
-    s_at_s, s_at_r, s_wo_s, s_wo_r, s_wp_s, s_wp_r,
+    s_at_s, s_at_r, s_wo_s, s_wo_r, s_wz_s, s_wz_r, s_wp_s, s_wp_r,
 ):
     s = lax.axis_index("seq")
     v = lax.axis_index("var")
@@ -76,11 +76,12 @@
                  (qkv_h.at[:, pl.ds(64, 128)], wkv.at[i]),
                  (up_h, wu.at[i]),
                  (dn_h, wd.at[i]))
+    mine = pl.ds(sz * 16, 16)
     loads = []
     for k, (a, b) in enumerate((
         (fields_h, fields), (kv_h, kv3), (emb, we.at[p]), (aquery_h, aquery), (vart_h, vart), (atemp_h, atemp),
         (aout_h, aout), (pos_h.at[pl.ds(v * 16, 16)], posv), (leadt_h, leadt), (gains_h, gains),
-        (fgain_h, fgain), (head_h.at[:, i], headp.at[:, pl.ds(0, 48)]), *own_heads, (wo_h, wo.at[:, v]),
+        (fgain_h, fgain), (head_h.at[:, i], headp.at[:, pl.ds(0, 48)]), *own_heads, (wo_h.at[:, mine], wo.at[:, p, i, mine]),
     )):
         loads.append(pltpu.make_async_copy(a, b, s_loc.at[k]))
     for c in loads[:6]:
@@ -114,25 +115,31 @@
     for c in init:
         c.start()
     wcopies = []
-    for k, (a, b) in enumerate((*own_heads, (wo_h, wo.at[:, v]))):
+    for k, (a, b) in enumerate(own_heads):
         wcopies.append(remote(a, b, s_ws.at[k], s_wr.at[k], other))
     for c in wcopies:
         c.start()
 
     def wo_copy(l, k):
-        return remote(wo_h.at[l], wo.at[l, v], s_wo_s.at[l, k], s_wo_r.at[l, k], var_dev(var_dst[k]))
+        return remote(wo_h.at[l, mine], wo.at[l, p, i, mine], s_wo_s.at[l, k], s_wo_r.at[l, k], var_dev(var_dst[k]))
 
     def wo_arrival(l, k):
-        h = var_src[k] * 2 + i
-        return remote(wo_h.at[l], wo.at[l, h], s_wo_s.at[l, k], s_wo_r.at[l, k], var_dev(var_dst[k]))
-
-    def wo_pass(l, k):
-        h = var_src[k] * 2 + i
-        return remote(wo.at[l, h], wo.at[l, h], s_wp_s.at[l, k], s_wp_r.at[l, k], other)
-
-    def wo_passed(l, k):
-        h = var_src[k] * 2 + 1 - i
-        return remote(wo.at[l, h], wo.at[l, h], s_wp_s.at[l, k], s_wp_r.at[l, k], other)
+        return remote(wo_h.at[l, mine], wo.at[l, var_src[k], i, mine], s_wo_s.at[l, k], s_wo_r.at[l, k],
+                      var_dev(var_dst[k]))
+
+    def wo_quarter(l, dz, back):
+        rows = pl.ds(((sz + 4 - dz) % 4) * 16, 16) if back else mine
+        quarter = wo.at[l, :, i, rows]
+        return remote(quarter, quarter, s_wz_s.at[l, dz - 1], s_wz_r.at[l, dz - 1], (((sz + dz) % 4) * 2 + sy, v))
+
+    def wo_pass(l, core):
+        return remote(wo.at[l, :, core], wo.at[l, :, core], s_wp_s.at[l], s_wp_r.at[l], other)
+
+    def wo_spread(l):
+        for k in range(7):
+            wo_arrival(l, k).wait_recv()
+        for dz in (2, 1, 3):
+            wo_quarter(l, dz, False).start()
 
     for k in range(7):
         wo_copy(0, k).start()
@@ -183,6 +190,8 @@
         c.wait_send()
     for c in loads[6:12]:
         c.wait()
+    loads[16].wait()
+    wo_spread(0)
 
     lane64 = lax.broadcasted_iota(jnp.int32, (32, 64), 1)
     lane128 = lax.broadcasted_iota(jnp.int32, (128, 128), 1)
@@ -248,12 +257,10 @@
 
         @pl.when(step == 0)
         def _():
-            for c in loads[12:]:
+            for c in loads[12:16]:
                 c.wait()
-            for c in wcopies[:4]:
+            for c in wcopies:
                 c.wait()
-            wcopies[4].wait_send()
-            remote(wo_h, wo.at[:, p * 2 + 1 - i], s_ws.at[4], s_wr.at[4], other).wait_recv()
 
         def layer_body(l, carry):
             x, cg = gather_rows(resid[...])
@@ -290,9 +297,9 @@
 
             @pl.when(step == 0)
             def _():
-                for k in range(7):
-                    wo_arrival(l, k).wait_recv()
-                    wo_pass(l, k).start()
+                for dz in (1, 2, 3):
+                    wo_quarter(l, dz, True).wait_recv()
+                wo_pass(l, i).start()
 
             for c in cg:
                 c.wait_send()
@@ -335,10 +342,12 @@
 
             @pl.when(step == 0)
             def _():
+                wo_pass(l, 1 - i).wait_recv()
+                wo_pass(l, i).wait_send()
                 for k in range(7):
-                    wo_passed(l, k).wait_recv()
-                    wo_pass(l, k).wait_send()
                     wo_copy(l, k).wait_send()
+                for dz in (1, 2, 3):
+                    wo_quarter(l, dz, False).wait_send()
 
             partner(ax.at[1 - i], ab.at[p * 2 + 1 - i], 3).wait_recv()
             for k in range(7):
@@ -353,6 +362,11 @@
                 at[pl.ds(64, 64), cols] = jnp.where(left, pltpu.roll(even, 64, 1), odd).astype(BF16)
             rows = rows + dot(at[...], wo[l].reshape(1024, 1024))
             rs[...] = rows.reshape(8, 16, 1024)
+
+            @pl.when((step == 0) & (l == 0))
+            def _():
+                wo_spread(1)
+
             x = layer_norm(rows, gains[l, pl.ds(1, 1), :]).astype(BF16)
             part = jnp.zeros((128, 1024), F32)
             for h in range(2):
@@ -424,7 +438,7 @@
             V((1024, 2, 1024), BF16),
             V((2, LAYERS, 128, 1024), BF16),
             V((2, LAYERS, 128, 1024), BF16),
-            V((LAYERS, 16, 64, 1024), BF16),
+            V((LAYERS, 8, 2, 64, 1024), BF16),
             V((2, LAYERS, 1024, 256), BF16),
             V((2, LAYERS, 256, 1024), BF16),
             V((1024, 2048), BF16),
@@ -469,7 +483,8 @@
             dma((STEPS, 7)), dma((STEPS, 7)),
             dma((14,)), dma((14,)),
             dma((LAYERS, 7)), dma((LAYERS, 7)),
-            dma((LAYERS, 7)), dma((LAYERS, 7)),
+            dma((LAYERS, 3)), dma((LAYERS, 3)),
+            dma((LAYERS,)), dma((LAYERS,)),
         ],
         compiler_params=pltpu.CompilerParams(
             collective_id=0, has_side_effects=True, vmem_limit_bytes=60 * 1024 * 1024

time: 162 us -> 153 us (0.944)
  Pallas kernels: 160 us -> 150 us
    pallas_call x1, Pallas kernels: 160 us -> 150 us  [per_device(): pl.pallas_call(kernel, out_shape=jax.ShapeDtypeStruct((STEPS, 48, 1, 256)...]
where the time goes in v4:
time: 153 us; the launch traced here: 152 us
  Pallas kernels  150 us (98%)
  local copies, waits for them, and re-layouts  1.54 us (1%)
    pallas_call x1, Pallas kernels, per_device(): pl.pallas_call(kernel, out_shape=jax.ShapeDtypeStruct((STEPS, 48, 1, 256)...  150 us

profile of v4, /device:TPU:1, one launch (start us, length us, event | category | flops | bytes accessed | tf_op | source)
XLA Modules:
  0.0 152.4 jit_solution(2777684654964774759)
XLA Ops:
  0.7 150.2 %rollout.1 = f32[2,48,1,256]{3,2,1,0:T(1,128)} custom-call(s32[3]{0:T(128)} %ids.1, s32[1]{0:T(128)S(6)} %copy.22.lead, f32[2]{0:T(128)} %bitcast.22, f32[48,1,256]{2,1,0:T(1,128)} %bitcast.20, bf16[48,1024]{1,0:T(8,128)(2,1)} %bitcast.19, bf16[48,1024]{1,0:T(8,128)(2,1)} %vart_h.1, bf16[16,64]{1,0:T(8,128)(2,1)} %aquery_h.1, bf16[1024,2,1024]{2,1,0:T(2,128)(2,1)} %kv_h.1, ...), custom_call_target="tpu_custom_call" | custom-call | tf_op jit(solution)/shard_map/rollout/pallas_call | solution.py:425
  150.8 1.5 %copy.23 = f32[2,3,16,1,256]{4,3,2,1,0:T(1,128)} copy(f32[2,3,16,1,256]{4,3,2,1,0:T(1,128)} %bitcast.17) | data formatting | bytes 196608

commit v5 on v4

--- a/solution.py
+++ b/solution.py
@@ -72,8 +72,8 @@
             src_ref=src, dst_ref=dst, send_sem=send, recv_sem=recv, device_id=dev, device_id_type=MESH
         )
 
-    own_heads = ((qkv_h.at[:, pl.ds(0, 64)], wq.at[i, :, pl.ds(0, 64)]),
-                 (qkv_h.at[:, pl.ds(64, 128)], wkv.at[i]),
+    own_heads = ((qkv_h.at[:, pl.ds(0, 64)], wq.at[:, i, pl.ds(0, 64)]),
+                 (qkv_h.at[:, pl.ds(64, 128)], wkv.at[:, i]),
                  (up_h, wu.at[i]),
                  (dn_h, wd.at[i]))
     mine = pl.ds(sz * 16, 16)
@@ -145,7 +145,7 @@
         wo_copy(0, k).start()
 
     st[p] = fsnd[p]
-    wq[:, :, pl.ds(64, 64)] = jnp.zeros((2, LAYERS, 64, 1024), BF16)
+    wq[:, :, pl.ds(64, 64)] = jnp.zeros((LAYERS, 2, 64, 1024), BF16)
     headp[:, pl.ds(48, 80)] = jnp.zeros((8, 80, 1024), BF16)
 
     hrow = lax.broadcasted_iota(jnp.int32, (128, 1024), 0)
@@ -194,32 +194,37 @@
     wo_spread(0)
 
     lane64 = lax.broadcasted_iota(jnp.int32, (32, 64), 1)
-    lane128 = lax.broadcasted_iota(jnp.int32, (128, 128), 1)
+    left64 = lax.broadcasted_iota(jnp.int32, (64, 128), 1) < 64
 
     def partner(src, dst, k):
         return remote(src, dst, s_px_s.at[k], s_px_r.at[k], other)
 
-    def gather_rows(own):
-        xg[p] = own.astype(BF16)
-        cs = [remote(xg.at[p], xg.at[p], s_ag_s.at[k], s_ag_r.at[k], var_dev(var_dst[k])) for k in range(7)]
-        for c in cs:
-            c.start()
+    def gather(c, k, src):
+        return remote(xg.at[c, p], xg.at[c, src], s_ag_s.at[c, k], s_ag_r.at[c, k], var_dev(var_dst[k]))
+
+    def start_gather(c, own):
+        xg[c, p] = own.astype(BF16)
         for k in range(7):
-            remote(xg.at[p], xg.at[var_src[k]], s_ag_s.at[k], s_ag_r.at[k], var_dev(var_dst[k])).wait_recv()
-        return xg[...].reshape(128, 1024), cs
-
-    def sum_rows(part):
-        pb[...] = part.astype(BF16).reshape(8, 16, 1024)
-        cs = [remote(pb.at[var_dst[k]], rsb.at[k], s_rs_s.at[k], s_rs_r.at[k], var_dev(var_dst[k])) for k in range(7)]
-        for c in cs:
-            c.start()
-        total = rs[p] + pb[p].astype(F32)
-        for k in (6, 5, 4, 3, 2, 1, 0):
-            cs[k].wait_recv()
-            total = total + rsb[k].astype(F32)
-        resid[...] = total
-        for c in cs:
-            c.wait_send()
+            gather(c, k, p).start()
+
+    def sums(c, k):
+        return remote(pb.at[c, var_dst[k]], rsb.at[c, k], s_rs_s.at[c, k], s_rs_r.at[c, k], var_dev(var_dst[k]))
+
+    def keys_out(l, c, k, h):
+        return remote(kvo.at[h, c], kvb.at[l, c, s, i], s_kv_s.at[c, 2 * k + h], s_kv_r.at[l, c, 2 * k + i],
+                      (seq_dst[k], p * 2 + h))
+
+    def keys_in(l, c, k, j):
+        return remote(kvo.at[j, c], kvb.at[l, c, seq_src[k], j], s_kv_s.at[c, 2 * k + j],
+                      s_kv_r.at[l, c, 2 * k + j], (seq_dst[k], p * 2 + j))
+
+    def mixed_out(c, k, j):
+        return remote(ax.at[j, c], ab.at[c, v], s_at_s.at[c, 2 * k + j], s_at_r.at[c, 2 * k + i],
+                      (s, var_dst[k] * 2 + j))
+
+    def mixed_in(c, k, j):
+        return remote(ax.at[j, c], ab.at[c, var_src[k] * 2 + j], s_at_s.at[c, 2 * k + j], s_at_r.at[c, 2 * k + j],
+                      (s, var_dst[k] * 2 + j))
 
     def step_body(step, carry):
         for q in range(8):
@@ -253,7 +258,9 @@
         tot = ndx[i] + ndr[...]
         pooled = (tot[:, :1024] / tot[:, 1024:]).astype(BF16)
         c.wait_send()
-        resid[...] = dot(pooled, aout[...]) + add
+        own = dot(pooled, aout[...]) + add
+        for n in range(2):
+            start_gather(n, own[8 * n : 8 * n + 8])
 
         @pl.when(step == 0)
         def _():
@@ -263,37 +270,33 @@
                 c.wait()
 
         def layer_body(l, carry):
-            x, cg = gather_rows(resid[...])
-
-            rows = x.astype(F32)
-            x = layer_norm(rows, gains[l, pl.ds(0, 1), :]).astype(BF16)
-            cs = []
-            for h in range(2):
-                kv = dot_t(x, wkv[h, l])
-                kq = jnp.where(lane128 < 64, kv * kv, 0.0)
-                scale = lax.rsqrt(jnp.sum(kq, axis=-1, keepdims=True) * (1.0 / 64.0) + EPS_UNIT)
-                kvo[h] = (kv * jnp.where(lane128 < 64, scale, 1.0)).astype(BF16)
-                for k in range(7):
-                    c = remote(kvo.at[h], kvb.at[l, s, i], s_kv_s.at[2 * k + h],
-                               s_kv_r.at[l, 2 * k + i], (seq_dst[k], p * 2 + h))
-                    c.start()
-                    cs.append(c)
-            ck = partner(kvo.at[1 - i], kvb.at[l, s, i], 2)
-            ck.start()
+            for n in range(2):
+                for k in range(7):
+                    gather(n, k, var_src[k]).wait_recv()
+                x = layer_norm(xg[n].astype(F32).reshape(64, 1024), gains[l, pl.ds(0, 1), :]).astype(BF16)
+                both = dot_t(x, wkv[l].reshape(256, 1024))
+                for h in range(2):
+                    kv = both[:, 128 * h : 128 * h + 128]
+                    kq = jnp.where(left64, kv * kv, 0.0)
+                    scale = lax.rsqrt(jnp.sum(kq, axis=-1, keepdims=True) * (1.0 / 64.0) + EPS_UNIT)
+                    kvo[h, n] = (kv * jnp.where(left64, scale, 1.0)).astype(BF16)
+                for k in range(7):
+                    for h in range(2):
+                        keys_out(l, n, k, h).start()
+                partner(kvo.at[1 - i, n], kvb.at[l, n, s, i], 5 + n).start()
+                kvb[l, n, s, i] = kvo[i, n]
+                both = dot_t(x, wq[l].reshape(256, 1024))
+                for h in range(2):
+                    q = both[:, 128 * h : 128 * h + 128]
+                    q = q * lax.rsqrt(jnp.sum(q * q, axis=-1, keepdims=True) * (1.0 / 64.0) + EPS_UNIT)
+                    qx[h, n] = q.astype(BF16)
+            partner(qx.at[1 - i], qb.at[i], 1).start()
+            qb[i] = qx[i]
 
             @pl.when((step == 0) & (l == 0))
             def _():
                 for k in range(7):
                     wo_copy(1, k).start()
-
-            for h in range(2):
-                q = dot_t(x, wq[h, l])
-                q = q * lax.rsqrt(jnp.sum(q * q, axis=-1, keepdims=True) * (1.0 / 64.0) + EPS_UNIT)
-                qx[h] = q.astype(BF16)
-            cq = partner(qx.at[1 - i], qb.at[i], 1)
-            cq.start()
-            qb[i] = qx[i]
-            kvb[l, s, i] = kvo[i]
 
             @pl.when(step == 0)
             def _():
@@ -301,44 +304,47 @@
                     wo_quarter(l, dz, True).wait_recv()
                 wo_pass(l, i).start()
 
-            for c in cg:
-                c.wait_send()
+            for n in range(2):
+                for k in range(7):
+                    gather(n, k, p).wait_send()
             partner(qx.at[1 - i], qb.at[1 - i], 1).wait_recv()
-            partner(kvo.at[1 - i], kvb.at[l, s, 1 - i], 2).wait_recv()
             scale = temp[l] * (1.0 / 64.0)
             q = qb[...].reshape(256, 128)
             num = jnp.zeros((256, 128), F32)
             den = jnp.zeros((256, 128), F32)
-            for k in (7, 6, 5, 4, 3, 2, 1, 0):
-                if k == 7:
-                    src = s
-                else:
-                    src = seq_src[k]
+            for n in range(2):
+                for pair in ((7, 6), (5, 4), (3, 2), (1, 0)):
+                    block = []
+                    for k in pair:
+                        if k == 7:
+                            partner(kvo.at[1 - i, n], kvb.at[l, n, s, 1 - i], 5 + n).wait_recv()
+                            block.append(kvb[l, n, s].reshape(128, 128))
+                        else:
+                            for j in range(2):
+                                keys_in(l, n, k, j).wait_recv()
+                            block.append(kvb[l, n, seq_src[k]].reshape(128, 128))
+                    kv = jnp.concatenate(block, axis=0)
+                    e = jnp.exp(dot_t(q, kv) * scale)
+                    den = den + e[:, :128] + e[:, 128:]
+                    num = num + dot(e.astype(BF16), kv)
+            att = num / jnp.sum(den, axis=-1, keepdims=True)
+            for n in range(2):
+                for h in range(2):
+                    r = 128 * h + 64 * n
+                    ax[h, n] = jnp.where(
+                        left64[:32], pltpu.roll(att[r : r + 32], 64, 1), att[r + 32 : r + 64]
+                    ).astype(BF16)
+                for k in range(7):
                     for j in range(2):
-                        remote(kvo.at[j], kvb.at[l, src, j], s_kv_s.at[2 * k + j],
-                               s_kv_r.at[l, 2 * k + j], (seq_dst[k], p * 2 + j)).wait_recv()
-                kv = kvb[l, src].reshape(256, 128)
-                e = jnp.exp(dot_t(q, kv) * scale)
-                den = den + e[:, :128] + e[:, 128:]
-                num = num + dot(e.astype(BF16), kv)
-            att = num / jnp.sum(den, axis=-1, keepdims=True)
-            for h in range(2):
-                lo, hi = att[128 * h : 128 * h + 64], att[128 * h + 64 : 128 * h + 128]
-                ax[h] = jnp.where(lane128[:64] < 64, pltpu.roll(lo, 64, 1), hi).astype(BF16)
-            ca = []
-            for k in range(7):
-                for j in range(2):
-                    ca.append(remote(ax.at[j], ab.at[v], s_at_s.at[2 * k + j], s_at_r.at[2 * k + i],
-                                     (s, var_dst[k] * 2 + j)))
-            for c in ca:
-                c.start()
-            cp = partner(ax.at[1 - i], ab.at[v], 3)
-            cp.start()
-            ab[v] = ax[i]
-            for c in cs:
-                c.wait_send()
-            cq.wait_send()
-            ck.wait_send()
+                        mixed_out(n, k, j).start()
+                partner(ax.at[1 - i, n], ab.at[n, v], 2 + n).start()
+                ab[n, v] = ax[i, n]
+            for n in range(2):
+                for k in range(7):
+                    for h in range(2):
+                        keys_out(l, n, k, h).wait_send()
+                partner(kvo.at[1 - i, n], kvb.at[l, n, s, i], 5 + n).wait_send()
+            partner(qx.at[1 - i], qb.at[i], 1).wait_send()
 
             @pl.when(step == 0)
             def _():
@@ -349,34 +355,49 @@
                 for dz in (1, 2, 3):
                     wo_quarter(l, dz, False).wait_send()
 
-            partner(ax.at[1 - i], ab.at[p * 2 + 1 - i], 3).wait_recv()
-            for k in range(7):
-                for j in range(2):
-                    remote(ax.at[j], ab.at[var_src[k] * 2 + j], s_at_s.at[2 * k + j], s_at_r.at[2 * k + j],
-                           (s, var_dst[k] * 2 + j)).wait_recv()
-            for q in range(8):
-                even, odd = ab[2 * q].astype(F32), ab[2 * q + 1].astype(F32)
-                cols = pl.ds(q * 128, 128)
-                left = lane128[:64] < 64
-                at[pl.ds(0, 64), cols] = jnp.where(left, even, pltpu.roll(odd, 64, 1)).astype(BF16)
-                at[pl.ds(64, 64), cols] = jnp.where(left, pltpu.roll(even, 64, 1), odd).astype(BF16)
-            rows = rows + dot(at[...], wo[l].reshape(1024, 1024))
-            rs[...] = rows.reshape(8, 16, 1024)
+            for n in range(2):
+                partner(ax.at[1 - i, n], ab.at[n, p * 2 + 1 - i], 2 + n).wait_recv()
+                for k in range(7):
+                    for j in range(2):
+                        mixed_in(n, k, j).wait_recv()
+                for q in range(8):
+                    even, odd = ab[n, 2 * q].astype(F32), ab[n, 2 * q + 1].astype(F32)
+                    cols = pl.ds(q * 128, 128)
+                    at[n, pl.ds(0, 32), cols] = jnp.where(left64[:32], even, pltpu.roll(odd, 64, 1)).astype(BF16)
+                    at[n, pl.ds(32, 32), cols] = jnp.where(left64[:32], pltpu.roll(even, 64, 1), odd).astype(BF16)
+                rows = xg[n].astype(F32).reshape(64, 1024) + dot(at[n], wo[l].reshape(1024, 1024))
+                rs[n] = rows.reshape(8, 8, 1024)
+                x = layer_norm(rows, gains[l, pl.ds(1, 1), :]).astype(BF16)
+                part = jnp.zeros((64, 1024), F32)
+                for h in range(2):
+                    hid = dot(x, wu[h, l])
+                    hid = 0.5 * hid * (1.0 + lax.erf(hid * (0.5 ** 0.5)))
+                    part = part + dot(hid.astype(BF16), wd[h, l])
+                pb[n] = part.reshape(8, 8, 1024).astype(BF16)
+                for k in range(7):
+                    sums(n, k).start()
 
             @pl.when((step == 0) & (l == 0))
             def _():
                 wo_spread(1)
 
-            x = layer_norm(rows, gains[l, pl.ds(1, 1), :]).astype(BF16)
-            part = jnp.zeros((128, 1024), F32)
-            for h in range(2):
-                hid = dot(x, wu[h, l])
-                hid = 0.5 * hid * (1.0 + lax.erf(hid * (0.5 ** 0.5)))
-                part = part + dot(hid.astype(BF16), wd[h, l])
-            for c in ca:
-                c.wait_send()
-            cp.wait_send()
-            sum_rows(part)
+            for n in range(2):
+                own = rs[n, p] + pb[n, p].astype(F32)
+                for k in (6, 5, 4, 3, 2, 1, 0):
+                    sums(n, k).wait_recv()
+                    own = own + rsb[n, k].astype(F32)
+
+                @pl.when(l < LAYERS - 1)
+                def _(n=n, own=own):
+                    start_gather(n, own)
+
+                resid[pl.ds(8 * n, 8), :] = own
+            for n in range(2):
+                for k in range(7):
+                    sums(n, k).wait_send()
+                    for j in range(2):
+                        mixed_out(n, k, j).wait_send()
+                partner(ax.at[1 - i, n], ab.at[n, v], 2 + n).wait_send()
             return carry
 
         lax.fori_loop(0, LAYERS, layer_body, 0)
@@ -436,8 +457,8 @@
             V((LAYERS, 2, 1024), F32),
             V((1, 1024), F32),
             V((1024, 2, 1024), BF16),
-            V((2, LAYERS, 128, 1024), BF16),
-            V((2, LAYERS, 128, 1024), BF16),
+            V((LAYERS, 2, 128, 1024), BF16),
+            V((LAYERS, 2, 128, 1024), BF16),
             V((LAYERS, 8, 2, 64, 1024), BF16),
             V((2, LAYERS, 1024, 256), BF16),
             V((2, LAYERS, 256, 1024), BF16),
@@ -458,17 +479,17 @@
             V((128, 1024), BF16),
             V((128, 1024), BF16),
             V((16, 1024), F32),
-            V((8, 16, 1024), BF16),
-            V((8, 16, 1024), BF16),
-            V((7, 16, 1024), BF16),
-            V((2, 128, 128), BF16),
-            V((2, 128, 128), BF16),
-            V((LAYERS, 8, 2, 128, 128), BF16),
-            V((2, 128, 128), BF16),
-            V((2, 64, 128), BF16),
-            V((16, 64, 128), BF16),
-            V((128, 1024), BF16),
-            V((8, 16, 1024), F32),
+            V((2, 8, 8, 1024), BF16),
+            V((2, 8, 8, 1024), BF16),
+            V((2, 7, 8, 1024), BF16),
+            V((2, 2, 64, 128), BF16),
+            V((2, 2, 64, 128), BF16),
+            V((LAYERS, 2, 8, 2, 64, 128), BF16),
+            V((2, 2, 64, 128), BF16),
+            V((2, 2, 32, 128), BF16),
+            V((2, 16, 32, 128), BF16),
+            V((2, 64, 1024), BF16),
+            V((2, 8, 8, 1024), F32),
             V((2, 16, 1024), BF16),
             V((STEPS, 8, 32, 128), BF16),
             V((STEPS, 8, 32, 128), BF16),
@@ -476,12 +497,12 @@
             dma((5,)), dma((5,)),
             dma((7,)), dma((7,)),
             dma((7,)), dma((7,)),
+            dma((2, 7)), dma((2, 7)),
+            dma((2, 7)), dma((2, 7)),
+            dma((2, 14)), dma((LAYERS, 2, 14)),
             dma((7,)), dma((7,)),
-            dma((7,)), dma((7,)),
-            dma((14,)), dma((LAYERS, 14)),
-            dma((5,)), dma((5,)),
             dma((STEPS, 7)), dma((STEPS, 7)),
-            dma((14,)), dma((14,)),
+            dma((2, 14)), dma((2, 14)),
             dma((LAYERS, 7)), dma((LAYERS, 7)),
             dma((LAYERS, 3)), dma((LAYERS, 3)),
             dma((LAYERS,)), dma((LAYERS,)),

time: 153 us -> 150 us (0.980)
  Pallas kernels: 150 us -> 148 us
    pallas_call x1, Pallas kernels: 150 us -> 148 us  [per_device(): pl.pallas_call(kernel, out_shape=jax.ShapeDtypeStruct((STEPS, 48, 1, 256)...]
where the time goes in v5:
time: 150 us
  Pallas kernels  148 us (99%)
  local copies, waits for them, and re-layouts  1.54 us (1%)
    pallas_call x1, Pallas kernels, per_device(): pl.pallas_call(kernel, out_shape=jax.ShapeDtypeStruct((STEPS, 48, 1, 256)...  148 us

profile of v5, /device:TPU:1, one launch (start us, length us, event | category | flops | bytes accessed | tf_op | source)
XLA Modules:
  0.0 150.3 jit_solution(79135941348272420)
XLA Ops:
  0.7 148.1 %rollout.1 = f32[2,48,1,256]{3,2,1,0:T(1,128)} custom-call(s32[3]{0:T(128)} %ids.1, s32[1]{0:T(128)S(6)} %copy.22.lead, f32[2]{0:T(128)} %bitcast.22, f32[48,1,256]{2,1,0:T(1,128)} %bitcast.20, bf16[48,1024]{1,0:T(8,128)(2,1)} %bitcast.19, bf16[48,1024]{1,0:T(8,128)(2,1)} %vart_h.1, bf16[16,64]{1,0:T(8,128)(2,1)} %aquery_h.1, bf16[1024,2,1024]{2,1,0:T(2,128)(2,1)} %kv_h.1, ...), custom_call_target="tpu_custom_call" | custom-call | tf_op jit(solution)/shard_map/rollout/pallas_call | solution.py:446
  148.8 1.5 %copy.23 = f32[2,3,16,1,256]{4,3,2,1,0:T(1,128)} copy(f32[2,3,16,1,256]{4,3,2,1,0:T(1,128)} %bitcast.17) | data formatting | bytes 196608

commit v6 on v5

--- a/solution.py
+++ b/solution.py
@@ -32,16 +32,16 @@
 
 
 def kernel(
-    ids, lead, temp, fields_h, emb, vart_h, aquery_h, kv_h, aout_h, atemp_h, pos_h, leadt_h, gains_h,
+    ids_h, lead_h, temp_h, fields_h, emb, vart_h, aquery_h, kv_h, aout_h, atemp_h, pos_h, leadt_h, gains_h,
     qkv_h, wo_h, up_h, dn_h, fgain_h, head_h,
     out,
-    fields, vart, aquery, atemp, leadt, gains, fgain, kv3,
+    ids, lead, temp, fields, vart, aquery, atemp, leadt, gains, fgain, kv3,
     wq, wkv, wo, wu, wd, kvv, aout, headp, posv,
-    fsnd, st, we, mb, kb, k2, vv, wb, ndx, ndr, hexp, qexp,
+    fsnd, st, we, mb, m0, n0, p0r, p0x, p0b, kb, k2, vv, wb, ndx, ndr, hexp, qexp,
     resid, xg, pb, rsb, qb, qx, kvb, kvo, ax, ab, at, rs, fb, db, dlr,
-    s_loc, s_ws, s_wr, s_is, s_ir, s_es, s_er, s_ag_s, s_ag_r, s_rs_s, s_rs_r,
+    s_loc, s_sc, s_ws, s_wr, s_is, s_ir, s_es, s_er, s_ag_s, s_ag_r, s_rs_s, s_rs_r,
     s_kv_s, s_kv_r, s_px_s, s_px_r, s_d_s, s_d_r,
-    s_at_s, s_at_r, s_wo_s, s_wo_r, s_wz_s, s_wz_r, s_wp_s, s_wp_r,
+    s_at_s, s_at_r, s_wo_s, s_wo_r, s_wz_s, s_wz_r, s_wp_s, s_wp_r, s_p0_s, s_p0_r,
 ):
     s = lax.axis_index("seq")
     v = lax.axis_index("var")
@@ -84,7 +84,9 @@
         (fgain_h, fgain), (head_h.at[:, i], headp.at[:, pl.ds(0, 48)]), *own_heads, (wo_h.at[:, mine], wo.at[:, p, i, mine]),
     )):
         loads.append(pltpu.make_async_copy(a, b, s_loc.at[k]))
-    for c in loads[:6]:
+    scalars = [pltpu.make_async_copy(a, b, s_sc.at[k])
+               for k, (a, b) in enumerate(((ids_h, ids), (lead_h, lead), (temp_h, temp)))]
+    for c in (*scalars, *loads[:6]):
         c.start()
 
     bar = pltpu.get_barrier_semaphore()
@@ -98,6 +100,7 @@
 
     for c in loads[6:]:
         c.start()
+    scalars[0].wait()
     loads[0].wait()
     state0 = fields[:, 0, :]
     frow = lax.broadcasted_iota(jnp.int32, (80, 256), 0)
@@ -106,19 +109,15 @@
     extra = jnp.where(frow == 0, named, 0).astype(F32)
     fsnd[...] = jnp.transpose(jnp.concatenate([state0, extra], axis=0)).reshape(8, 32, 128)
 
-    pl.semaphore_wait(bar, 29)
-
-    init = []
-    for k in range(7):
-        init.append(remote(fsnd.at[var_dst[k]], st.at[p], s_is.at[k], s_ir.at[k], var_dev(var_dst[k])))
-        init.append(remote(emb, we.at[p], s_es.at[k], s_er.at[k], var_dev(var_dst[k])))
-    for c in init:
-        c.start()
+    def emb_copy(k, src):
+        return remote(emb, we.at[src], s_es.at[k], s_er.at[k], var_dev(var_dst[k]))
+
+    def field_copy(k, src):
+        return remote(fsnd.at[var_dst[k]], st.at[src], s_is.at[k], s_ir.at[k], var_dev(var_dst[k]))
+
     wcopies = []
     for k, (a, b) in enumerate(own_heads):
         wcopies.append(remote(a, b, s_ws.at[k], s_wr.at[k], other))
-    for c in wcopies:
-        c.start()
 
     def wo_copy(l, k):
         return remote(wo_h.at[l, mine], wo.at[l, p, i, mine], s_wo_s.at[l, k], s_wo_r.at[l, k], var_dev(var_dst[k]))
@@ -141,8 +140,13 @@
         for dz in (2, 1, 3):
             wo_quarter(l, dz, False).start()
 
+
+    pl.semaphore_wait(bar, 29)
+    for c in wcopies:
+        c.start()
     for k in range(7):
         wo_copy(0, k).start()
+    emb_copy(0, p).start()
 
     st[p] = fsnd[p]
     wq[:, :, pl.ds(64, 64)] = jnp.zeros((LAYERS, 2, 64, 1024), BF16)
@@ -170,28 +174,35 @@
 
     lax.fori_loop(0, 16, split_kv, 0)
     loads[2].wait()
-    for k in range(7):
-        remote(fsnd.at[0], st.at[var_src[k]], s_is.at[k], s_ir.at[k], var_dev(var_dst[k])).wait_recv()
-    nrow = lax.broadcasted_iota(jnp.int32, (128, 48), 0) % 16
-    ncol = lax.broadcasted_iota(jnp.int32, (128, 48), 1).astype(F32)
-    named = st[:, pl.ds(0, 16)].reshape(128, 128)[:, 48:49]
-    hot = jnp.where((named == ncol) & (nrow < 3), 1.0, 0.0).astype(BF16)
-    vall = dot(hot, vart[...]).astype(BF16)
+    hrow16 = lax.broadcasted_iota(jnp.int32, (16, 48), 0)
+    hcol16 = lax.broadcasted_iota(jnp.int32, (16, 48), 1)
+    idv = jnp.where(hrow16 == 0, ids[0], jnp.where(hrow16 == 1, ids[1], ids[2]))
+    hot = jnp.where((idv == hcol16) & (hrow16 < 3), 1.0, 0.0).astype(BF16)
+    lhs = jnp.concatenate([we[p], dot(hot, vart[...]).astype(BF16)], axis=0)
     for n in range(4):
         cols = pl.ds(n * 512, 512)
-        mb[:, pl.ds(48, 16), cols] = dot(vall, kvv[:, cols]).astype(BF16).reshape(8, 16, 512)
-    for k in range(7):
-        remote(emb, we.at[var_src[k]], s_es.at[k], s_er.at[k], var_dev(var_dst[k])).wait_recv()
-    wall = we[...].reshape(384, 1024)
-    for n in range(4):
-        cols = pl.ds(n * 512, 512)
-        mb[:, pl.ds(0, 48), cols] = dot(wall, kvv[:, cols]).astype(BF16).reshape(8, 48, 512)
-    for c in init:
-        c.wait_send()
-    for c in loads[6:12]:
-        c.wait()
-    loads[16].wait()
-    wo_spread(0)
+        m0[:, cols] = dot(lhs, kvv[:, cols]).astype(BF16)
+
+    def all_channels():
+        for k in range(7):
+            field_copy(k, var_src[k]).wait_recv()
+        nrow = lax.broadcasted_iota(jnp.int32, (128, 48), 0) % 16
+        ncol = lax.broadcasted_iota(jnp.int32, (128, 48), 1).astype(F32)
+        named = st[:, pl.ds(0, 16)].reshape(128, 128)[:, 48:49]
+        hot = jnp.where((named == ncol) & (nrow < 3), 1.0, 0.0).astype(BF16)
+        vall = dot(hot, vart[...]).astype(BF16)
+        for n in range(4):
+            cols = pl.ds(n * 512, 512)
+            mb[:, pl.ds(48, 16), cols] = dot(vall, kvv[:, cols]).astype(BF16).reshape(8, 16, 512)
+        for k in range(7):
+            emb_copy(k, var_src[k]).wait_recv()
+        wall = we[...].reshape(384, 1024)
+        for n in range(4):
+            cols = pl.ds(n * 512, 512)
+            mb[:, pl.ds(0, 48), cols] = dot(wall, kvv[:, cols]).astype(BF16).reshape(8, 48, 512)
+        for k in range(7):
+            field_copy(k, p).wait_send()
+            emb_copy(k, p).wait_send()
 
     lane64 = lax.broadcasted_iota(jnp.int32, (32, 64), 1)
     left64 = lax.broadcasted_iota(jnp.int32, (64, 128), 1) < 64
@@ -226,48 +237,87 @@
         return remote(ax.at[j, c], ab.at[c, var_src[k] * 2 + j], s_at_s.at[c, 2 * k + j], s_at_r.at[c, 2 * k + j],
                       (s, var_dst[k] * 2 + j))
 
-    def step_body(step, carry):
+    def pool_products(blocks, mat):
         for q in range(8):
-            sb = st[q][:, :64]
+            sb = blocks[q][:, :64]
             blk = jnp.concatenate(
                 [jnp.where(lane64 // 16 == n, sb, jnp.where(lane64 == 48 + n, 1.0, 0.0)) for n in range(3)], axis=0
             ).astype(BF16)
-            kk = dot(blk, mb[q, :, pl.ds(0, 1024)])
+            kk = dot(blk, mat(q, pl.ds(0, 1024)))
             kb[q] = kk.astype(BF16)
             k2[q] = (kk * kk).astype(BF16)
-            vv[q] = dot(blk, mb[q, :, pl.ds(1024, 1024)]).astype(BF16)
+            vv[q] = dot(blk, mat(q, pl.ds(1024, 1024))).astype(BF16)
         ss = dot_t(k2[...].reshape(768, 1024), hexp[...])
         qk = dot_t(kb[...].reshape(768, 1024), qexp[...])
         w = jnp.exp(qk * lax.rsqrt(ss * (1.0 / 64.0) + EPS_UNIT) * tvec)
         wb[...] = w.astype(BF16).reshape(8, 96, 128)
-        num = jnp.zeros((32, 1024), F32)
-        den = jnp.zeros((32, 1024), F32)
-        for q in range(8):
-            wx = dot(wb[q], hexp[...])
-            nx = wx * vv[q].astype(F32)
-            num = num + (nx[0:32] + nx[32:64] + nx[64:96])
-            den = den + (wx[0:32] + wx[32:64] + wx[64:96])
-        ndx[:, :, pl.ds(0, 1024)] = num.reshape(2, 16, 1024)
-        ndx[:, :, pl.ds(1024, 1024)] = den.reshape(2, 16, 1024)
-        c = partner(ndx.at[1 - i], ndr, 0)
-        c.start()
+
+    def start_rows(pooled, step):
         row16 = lax.broadcasted_iota(jnp.int32, (16, 16), 1)
         lhot = jnp.where(row16 == lead[0] + step, 1.0, 0.0).astype(BF16)
         add = posv[...].astype(F32) + dot(lhot, leadt[...])
-        c.wait_recv()
-        tot = ndx[i] + ndr[...]
-        pooled = (tot[:, :1024] / tot[:, 1024:]).astype(BF16)
-        c.wait_send()
-        own = dot(pooled, aout[...]) + add
+        own = dot(pooled.astype(BF16), aout[...]) + add
         for n in range(2):
             start_gather(n, own[8 * n : 8 * n + 8])
 
-        @pl.when(step == 0)
+    pool_products(fsnd, lambda q, cols: m0[:, cols])
+    for q in range(8):
+        wx = dot(wb[q], hexp[...])
+        nx = wx * vv[q].astype(F32)
+        wq3 = wb[q].astype(F32)
+        n0[:, q, :, pl.ds(0, 1024)] = (nx[0:32] + nx[32:64] + nx[64:96]).reshape(2, 16, 1024).astype(BF16)
+        n0[:, q, :, pl.ds(1024, 128)] = (wq3[0:32] + wq3[32:64] + wq3[64:96]).reshape(2, 16, 128).astype(BF16)
+    c0 = partner(n0.at[1 - i], p0r, 7)
+    c0.start()
+    for c in loads[6:12]:
+        c.wait()
+    loads[16].wait()
+    c0.wait_recv()
+    p0x[...] = (n0[i].astype(F32) + p0r[...].astype(F32)).astype(BF16)
+
+    def pool_sums(k):
+        return remote(p0x.at[var_dst[k]], p0b.at[k], s_p0_s.at[k], s_p0_r.at[k], var_dev(var_dst[k]))
+
+    for k in range(7):
+        pool_sums(k).start()
+    wo_spread(0)
+    for c in scalars[1:]:
+        c.wait()
+    tot = p0x[p].astype(F32)
+    for k in (6, 5, 4, 3, 2, 1, 0):
+        pool_sums(k).wait_recv()
+        tot = tot + p0b[k].astype(F32)
+    inv = 1.0 / tot[:, 1024:]
+    inv_hi = inv.astype(BF16)
+    inv_lo = (inv - inv_hi.astype(F32)).astype(BF16)
+    start_rows(tot[:, :1024] * (dot(inv_hi, hexp[...]) + dot(inv_lo, hexp[...])), 0)
+    c0.wait_send()
+    for k in range(7):
+        pool_sums(k).wait_send()
+    for c in loads[12:16]:
+        c.wait()
+    for c in wcopies:
+        c.wait()
+
+    def step_body(step, carry):
+        @pl.when(step == 1)
         def _():
-            for c in loads[12:16]:
-                c.wait()
-            for c in wcopies:
-                c.wait()
+            pool_products(st, lambda q, cols: mb[q, :, cols])
+            num = jnp.zeros((32, 1024), F32)
+            den = jnp.zeros((32, 1024), F32)
+            for q in range(8):
+                wx = dot(wb[q], hexp[...])
+                nx = wx * vv[q].astype(F32)
+                num = num + (nx[0:32] + nx[32:64] + nx[64:96])
+                den = den + (wx[0:32] + wx[32:64] + wx[64:96])
+            ndx[:, :, pl.ds(0, 1024)] = num.reshape(2, 16, 1024)
+            ndx[:, :, pl.ds(1024, 1024)] = den.reshape(2, 16, 1024)
+            c = partner(ndx.at[1 - i], ndr, 0)
+            c.start()
+            c.wait_recv()
+            tot = ndx[i] + ndr[...]
+            start_rows(tot[:, :1024] / tot[:, 1024:], 1)
+            c.wait_send()
 
         def layer_body(l, carry):
             for n in range(2):
@@ -297,6 +347,15 @@
             def _():
                 for k in range(7):
                     wo_copy(1, k).start()
+                for k in (1, 2, 3):
+                    emb_copy(k, p).start()
+
+            @pl.when((step == 0) & (l == 1))
+            def _():
+                for k in (4, 5, 6):
+                    emb_copy(k, p).start()
+                for k in range(7):
+                    field_copy(k, p).start()
 
             @pl.when(step == 0)
             def _():
@@ -354,6 +413,10 @@
                     wo_copy(l, k).wait_send()
                 for dz in (1, 2, 3):
                     wo_quarter(l, dz, False).wait_send()
+
+            @pl.when((step == 0) & (l == 1))
+            def _():
+                all_channels()
 
             for n in range(2):
                 partner(ax.at[1 - i, n], ab.at[n, p * 2 + 1 - i], 2 + n).wait_recv()
@@ -437,7 +500,6 @@
     up_weight, down_weight, final_gain, head_weight,
 ):
     vm = pl.BlockSpec(memory_space=pltpu.VMEM)
-    sm = pl.BlockSpec(memory_space=pltpu.SMEM)
     hb = pl.BlockSpec(memory_space=pl.ANY)
     dma = pltpu.SemaphoreType.DMA
     V = pltpu.VMEM
@@ -446,9 +508,12 @@
     out = pl.pallas_call(
         kernel,
         out_shape=jax.ShapeDtypeStruct((STEPS, 48, 1, 256), F32),
-        in_specs=[sm] * 3 + [hb] * 16,
+        in_specs=[hb] * 19,
         out_specs=vm,
         scratch_shapes=[
+            pltpu.SMEM((3,), jnp.int32),
+            pltpu.SMEM((1,), jnp.int32),
+            pltpu.SMEM((LAYERS,), F32),
             V((48, 1, 256), F32),
             V((48, 1024), BF16),
             V((16, 64), BF16),
@@ -470,6 +535,11 @@
             V((8, 32, 128), F32),
             V((8, 48, 1024), BF16),
             V((8, 64, 2048), BF16),
+            V((64, 2048), BF16),
+            V((2, 8, 16, 1152), BF16),
+            V((8, 16, 1152), BF16),
+            V((8, 16, 1152), BF16),
+            V((7, 16, 1152), BF16),
             V((8, 96, 1024), BF16),
             V((8, 96, 1024), BF16),
             V((8, 96, 1024), BF16),
@@ -494,18 +564,20 @@
             V((STEPS, 8, 32, 128), BF16),
             V((STEPS, 8, 32, 128), BF16),
             dma((17,)),
+            dma((3,)),
             dma((5,)), dma((5,)),
             dma((7,)), dma((7,)),
             dma((7,)), dma((7,)),
             dma((2, 7)), dma((2, 7)),
             dma((2, 7)), dma((2, 7)),
             dma((2, 14)), dma((LAYERS, 2, 14)),
-            dma((7,)), dma((7,)),
+            dma((8,)), dma((8,)),
             dma((STEPS, 7)), dma((STEPS, 7)),
             dma((2, 14)), dma((2, 14)),
             dma((LAYERS, 7)), dma((LAYERS, 7)),
             dma((LAYERS, 3)), dma((LAYERS, 3)),
             dma((LAYERS,)), dma((LAYERS,)),
+            dma((7,)), dma((7,)),
         ],
         compiler_params=pltpu.CompilerParams(
             collective_id=0, has_side_effects=True, vmem_limit_bytes=60 * 1024 * 1024

time: 150 us -> 145 us (0.967)
  Pallas kernels: 148 us -> 143 us
    pallas_call x1, Pallas kernels: 148 us -> 143 us  [per_device(): pl.pallas_call(kernel, out_shape=jax.ShapeDtypeStruct((STEPS, 48, 1, 256)...]
where the time goes in v6:
time: 145 us
  Pallas kernels  143 us (99%)
  local copies, waits for them, and re-layouts  1.54 us (1%)
    pallas_call x1, Pallas kernels, per_device(): pl.pallas_call(kernel, out_shape=jax.ShapeDtypeStruct((STEPS, 48, 1, 256)...  143 us

profile of v6, /device:TPU:1, one launch (start us, length us, event | category | flops | bytes accessed | tf_op | source)
XLA Modules:
  0.0 144.9 jit_solution(14401287507780959085)
XLA Ops:
  0.7 142.7 %rollout.1 = f32[2,48,1,256]{3,2,1,0:T(1,128)} custom-call(s32[3]{0:T(128)} %ids_h.1, s32[1]{0:T(128)S(6)} %copy.22.lead_h, f32[2]{0:T(128)} %bitcast.22, f32[48,1,256]{2,1,0:T(1,128)} %bitcast.20, bf16[48,1024]{1,0:T(8,128)(2,1)} %bitcast.19, bf16[48,1024]{1,0:T(8,128)(2,1)} %vart_h.1, bf16[16,64]{1,0:T(8,128)(2,1)} %aquery_h.1, ...), custom_call_target="tpu_custom_call" | custom-call | tf_op jit(solution)/shard_map/rollout/pallas_call | solution.py:508
  143.4 1.5 %copy.23 = f32[2,3,16,1,256]{4,3,2,1,0:T(1,128)} copy(f32[2,3,16,1,256]{4,3,2,1,0:T(1,128)} %bitcast.17) | data formatting | bytes 196608

commit v7 on v6

--- a/solution.py
+++ b/solution.py
@@ -144,9 +144,9 @@
     pl.semaphore_wait(bar, 29)
     for c in wcopies:
         c.start()
-    for k in range(7):
-        wo_copy(0, k).start()
-    emb_copy(0, p).start()
+    for l in range(LAYERS):
+        for k in range(7):
+            wo_copy(l, k).start()
 
     st[p] = fsnd[p]
     wq[:, :, pl.ds(64, 64)] = jnp.zeros((LAYERS, 2, 64, 1024), BF16)
@@ -345,14 +345,12 @@
 
             @pl.when((step == 0) & (l == 0))
             def _():
-                for k in range(7):
-                    wo_copy(1, k).start()
-                for k in (1, 2, 3):
+                for k in (0, 1, 3, 5):
                     emb_copy(k, p).start()
 
             @pl.when((step == 0) & (l == 1))
             def _():
-                for k in (4, 5, 6):
+                for k in (2, 4, 6):
                     emb_copy(k, p).start()
                 for k in range(7):
                     field_copy(k, p).start()
@@ -398,6 +396,10 @@
                         mixed_out(n, k, j).start()
                 partner(ax.at[1 - i, n], ab.at[n, v], 2 + n).start()
                 ab[n, v] = ax[i, n]
+            @pl.when((step == 0) & (l == 0))
+            def _():
+                wo_spread(1)
+
             for n in range(2):
                 for k in range(7):
                     for h in range(2):
@@ -439,10 +441,6 @@
                 pb[n] = part.reshape(8, 8, 1024).astype(BF16)
                 for k in range(7):
                     sums(n, k).start()
-
-            @pl.when((step == 0) & (l == 0))
-            def _():
-                wo_spread(1)
 
             for n in range(2):
                 own = rs[n, p] + pb[n, p].astype(F32)

time: 145 us -> 142 us (0.979)
  Pallas kernels: 143 us -> 140 us
    pallas_call x1, Pallas kernels: 143 us -> 140 us  [per_device(): pl.pallas_call(kernel, out_shape=jax.ShapeDtypeStruct((STEPS, 48, 1, 256)...]
where the time goes in v7:
time: 142 us
  Pallas kernels  140 us (99%)
  local copies, waits for them, and re-layouts  1.54 us (1%)
    pallas_call x1, Pallas kernels, per_device(): pl.pallas_call(kernel, out_shape=jax.ShapeDtypeStruct((STEPS, 48, 1, 256)...  140 us

profile of v7, /device:TPU:1, one launch (start us, length us, event | category | flops | bytes accessed | tf_op | source)
XLA Modules:
  0.0 142.2 jit_solution(17010797275196410753)
XLA Ops:
  0.7 140.0 %rollout.1 = f32[2,48,1,256]{3,2,1,0:T(1,128)} custom-call(s32[3]{0:T(128)} %ids_h.1, s32[1]{0:T(128)S(6)} %copy.22.lead_h, f32[2]{0:T(128)} %bitcast.22, f32[48,1,256]{2,1,0:T(1,128)} %bitcast.20, bf16[48,1024]{1,0:T(8,128)(2,1)} %bitcast.19, bf16[48,1024]{1,0:T(8,128)(2,1)} %vart_h.1, bf16[16,64]{1,0:T(8,128)(2,1)} %aquery_h.1, ...), custom_call_target="tpu_custom_call" | custom-call | tf_op jit(solution)/shard_map/rollout/pallas_call | solution.py:506
  140.7 1.5 %copy.23 = f32[2,3,16,1,256]{4,3,2,1,0:T(1,128)} copy(f32[2,3,16,1,256]{4,3,2,1,0:T(1,128)} %bitcast.17) | data formatting | bytes 196608
